TPU v7x, 32 devices: a whole 2x2x4 slice. The times are simulated.
32 devices in a mesh: frame: 4 (over y, x), row: 8 (over z, core).
Axes of the slice: x: 2, y: 2, z: 4, core: 2. Of those that a mesh axis runs over, the one named last changes fastest.
Arguments:
- tokens: bfloat16 [1, 32, 16, 16, 1024], P(None, 'frame', 'row'), may hold values from -6 to 6
- timesteps: int32 [1, 32], P(None, 'frame'), may hold values from 0 to 999, as said below
- noise_table: bfloat16 [1000, 1024], replicated, may hold values from -5 to 5
- mod_weight: bfloat16 [1024, 6144], P(None, 'row'), may hold values from -0.1875 to 0.1875
- mod_bias: bfloat16 [6144], P('row'), may hold values from -3 to 3
- attn_in: bfloat16 [1024, 4096], P('row'), may hold values from -0.1875 to 0.1875
- out_weight: bfloat16 [1024, 1024], P('row'), may hold values from -4 to 4
- up_weight: bfloat16 [1024, 4096], P('row'), may hold values from -0.1875 to 0.1875
- down_weight: bfloat16 [1024, 4096], P('row'), may hold values from -0.09375 to 0.09375
- cotangent: bfloat16 [1, 32, 16, 16, 1024], P(None, 'frame', 'row'), may hold values from -6 to 6
Outputs:
- mixed: bfloat16 [1, 32, 16, 16, 1024], P(None, 'frame', 'row')
- tokens_grad: bfloat16 [1, 32, 16, 16, 1024], P(None, 'frame', 'row')
- noise_table_grad: float32 [1000, 1024], replicated
- mod_weight_grad: float32 [1024, 6144], P(None, 'row')
- mod_bias_grad: float32 [6144], P('row')
- attn_in_grad: float32 [1024, 4096], P('row')
- out_weight_grad: float32 [1024, 1024], P('row')
- up_weight_grad: float32 [1024, 4096], P('row')
- down_weight_grad: float32 [1024, 4096], P('row')
Inputs may be any that keep to these rules, and one draw needn't show every extreme that they name: `timesteps`: Noise-level index of each frame; both 0 and 999 occur in every draw.
All inputs are finite; a program needn't handle non-finite values.
Results may differ from a plain program's by a relative error of at most 0.019.
The roundings to bfloat16 on the way count: a program that leaves them out, or rounds other values in their place, can miss the bound.
Values may be sent and summed in bfloat16 or wider, within the bound.
A program may use at most 576 MiB of HBM per device.

v0:
```python
from functools import partial
import math

import jax
import jax.numpy as jnp
import numpy as np
from jax import lax
from jax.sharding import PartitionSpec as P

HEADS = 16


EPS = 1e-06


def rotary_freqs(pair_count):
    third_count = pair_count // 3
    group_sizes = [pair_count - 2 * third_count, third_count, third_count]
    tables = []
    offset = 0
    for group_index in range(3):
        freq_table = np.zeros((pair_count,), np.float32)
        for inner_index in range(group_sizes[group_index]):
            freq_table[offset + inner_index] = 10000.0 ** (-inner_index / group_sizes[group_index])
        offset += group_sizes[group_index]
        tables.append(freq_table)
    return tables


def rotary_angles(frame_pos, row_pos, col_pos, pair_count):
    frame_freq, row_freq, col_freq = rotary_freqs(pair_count)
    return (
        frame_pos[..., None] * frame_freq
        + row_pos[..., None] * row_freq
        + col_pos[..., None] * col_freq
    )


def rotate(values, cosines, sines):
    half_dim = values.shape[-1] // 2
    upper_half = values[..., :half_dim]
    lower_half = values[..., half_dim:]
    return jnp.concatenate(
        [upper_half * cosines - lower_half * sines, upper_half * sines + lower_half * cosines],
        axis=-1,
    )


def layer_norm(values):
    row_mean = jnp.mean(values, axis=-1, keepdims=True)
    centered = values - row_mean
    row_var = jnp.mean(centered * centered, axis=-1, keepdims=True)
    return centered * lax.rsqrt(row_var + EPS)


def modulate(values, shift, scale_part):
    return layer_norm(values) * (1.0 + scale_part) + shift


def heads_first(tensor):
    return jnp.transpose(tensor, (3, 0, 1, 2, 4)).reshape(tensor.shape[3], -1, tensor.shape[4])


def heads_back(tensor, frame_count, grid_side):
    head_count, head_size = (tensor.shape[0], tensor.shape[2])
    shaped = tensor.reshape(head_count, frame_count, grid_side, grid_side, head_size)
    return jnp.transpose(shaped, (1, 2, 3, 0, 4))


def contract_rows(left_side, right_side):
    return lax.dot_general(
        left_side, right_side, (((0,), (0,)), ((), ())), preferred_element_type=jnp.float32
    )


def contract_last(left_side, right_side):
    return lax.dot_general(
        left_side, right_side, (((1,), (1,)), ((), ())), preferred_element_type=jnp.float32
    )


def block_split(tensor, block_size):
    return tensor.reshape((tensor.shape[0] // block_size, block_size) + tensor.shape[1:])


def block_join(tensor):
    return tensor.reshape((-1,) + tensor.shape[2:])


def clip_forward(allowed, score_scale, clip_items):
    query_clip, key_clip, value_clip = clip_items
    frame_count, grid_side = (query_clip.shape[0], query_clip.shape[1])
    query_head = heads_first(query_clip)
    key_head = heads_first(key_clip)
    value_head = heads_first(value_clip)
    scores = (
        jnp.einsum("hqd,hkd->hqk", query_head, key_head, preferred_element_type=jnp.float32)
        * score_scale
    )
    scores = jnp.where(allowed, scores, -1e30)
    log_total = jax.nn.logsumexp(scores, axis=-1)
    prob_low = jnp.exp(scores - log_total[..., None]).astype(jnp.bfloat16)
    attended = jnp.einsum("hqk,hkd->hqd", prob_low, value_head, preferred_element_type=jnp.float32)
    return (heads_back(attended.astype(jnp.bfloat16), frame_count, grid_side), log_total)


def clip_backward(allowed, score_scale, clip_items):
    query_clip, key_clip, value_clip, grad_clip, log_total = clip_items
    frame_count, grid_side = (query_clip.shape[0], query_clip.shape[1])
    key_frames = key_clip.shape[0]
    query_head = heads_first(query_clip)
    key_head = heads_first(key_clip)
    value_head = heads_first(value_clip)
    grad_head = heads_first(grad_clip)
    scores = (
        jnp.einsum("hqd,hkd->hqk", query_head, key_head, preferred_element_type=jnp.float32)
        * score_scale
    )
    scores = jnp.where(allowed, scores, -1e30)
    prob_values = jnp.exp(scores - log_total[..., None])
    prob_low = prob_values.astype(jnp.bfloat16)
    grad_value = jnp.einsum("hqk,hqd->hkd", prob_low, grad_head, preferred_element_type=jnp.float32)
    grad_probs = jnp.einsum(
        "hqd,hkd->hqk", grad_head, value_head, preferred_element_type=jnp.float32
    )
    row_inner = jnp.sum(prob_values * grad_probs, axis=-1, keepdims=True)
    grad_scores = (prob_values * (grad_probs - row_inner)).astype(jnp.bfloat16)
    grad_query = (
        jnp.einsum("hqk,hkd->hqd", grad_scores, key_head, preferred_element_type=jnp.float32)
        * score_scale
    )
    grad_key = (
        jnp.einsum("hqk,hqd->hkd", grad_scores, query_head, preferred_element_type=jnp.float32)
        * score_scale
    )
    return (
        heads_back(grad_query, frame_count, grid_side),
        heads_back(grad_key, key_frames, grid_side),
        heads_back(grad_value, key_frames, grid_side),
    )


def on_device(
    tokens,
    timesteps,
    noise_table,
    mod_weight,
    mod_bias,
    attn_in,
    out_weight,
    up_weight,
    down_weight,
    cotangent,
):
    clip_count, seg_frames, rows_dev, grid_side, model_width = tokens.shape
    head_dim = model_width // HEADS
    pair_count = head_dim // 2
    frame_index = lax.axis_index("frame")
    row_index = lax.axis_index("row")
    clip_len = seg_frames * lax.axis_size("frame")
    token_count = clip_count * seg_frames * rows_dev * grid_side
    per_frame = grid_side * grid_side
    score_scale = head_dim ** (-0.5)
    step_count = noise_table.shape[0]
    steps_iota = lax.broadcasted_iota(jnp.int32, (1, 1, step_count), 2)
    one_hot = (timesteps[:, :, None] == steps_iota).astype(jnp.bfloat16)
    embedding = jnp.einsum("cls,sd->cld", one_hot, noise_table, preferred_element_type=jnp.float32)
    silu_embed, silu_pull = jax.vjp(jax.nn.silu, embedding)
    silu_low = silu_embed.astype(jnp.bfloat16)
    mod_local = jnp.einsum(
        "cld,de->cle", silu_low, mod_weight, preferred_element_type=jnp.float32
    ) + mod_bias.astype(jnp.float32)
    modulation = lax.all_gather(mod_local.astype(jnp.bfloat16), "row", axis=2, tiled=True).astype(
        jnp.float32
    )
    modulation = modulation.reshape(clip_count, seg_frames, 6, 1, 1, model_width)
    shift_one = modulation[:, :, 0]
    scale_one = modulation[:, :, 1]
    gate_one = modulation[:, :, 2]
    shift_two = modulation[:, :, 3]
    scale_two = modulation[:, :, 4]
    gate_two = modulation[:, :, 5]
    full_in, full_out, full_up, full_down = (
        lax.all_gather(attn_in, "row", axis=0, tiled=True),
        lax.all_gather(out_weight, "row", axis=0, tiled=True),
        lax.all_gather(up_weight, "row", axis=0, tiled=True),
        lax.all_gather(down_weight, "row", axis=0, tiled=True),
    )
    token_f = tokens.astype(jnp.float32)
    hidden_one, norm_one_pull = jax.vjp(modulate, token_f, shift_one, scale_one)
    hidden_low = hidden_one.astype(jnp.bfloat16).reshape(token_count, model_width)
    mixed_in = jnp.dot(hidden_low, full_in, preferred_element_type=jnp.float32)
    query_raw = mixed_in[:, :model_width].reshape(token_count, HEADS, head_dim)
    key_raw = mixed_in[:, model_width : 2 * model_width].reshape(token_count, HEADS, head_dim)
    value_raw = mixed_in[:, 2 * model_width : 3 * model_width]
    gate_raw = mixed_in[:, 3 * model_width :]
    shape_four = (clip_count, seg_frames, rows_dev, grid_side)
    frame_pos = (frame_index * seg_frames + lax.broadcasted_iota(jnp.int32, shape_four, 1)).astype(
        jnp.float32
    )
    row_pos = (row_index * rows_dev + lax.broadcasted_iota(jnp.int32, shape_four, 2)).astype(
        jnp.float32
    )
    col_pos = lax.broadcasted_iota(jnp.float32, shape_four, 3)
    angles = rotary_angles(frame_pos, row_pos, col_pos, pair_count).reshape(
        token_count, 1, pair_count
    )
    cosines = jnp.cos(angles)
    sines = jnp.sin(angles)
    head_shape = (clip_count, seg_frames, rows_dev, grid_side, HEADS, head_dim)
    query_low = rotate(query_raw, cosines, sines).astype(jnp.bfloat16).reshape(head_shape)
    key_low = rotate(key_raw, cosines, sines).astype(jnp.bfloat16).reshape(head_shape)
    value_low = value_raw.astype(jnp.bfloat16).reshape(head_shape)
    mask_shape = (seg_frames * per_frame, clip_len * per_frame)
    query_frame = (
        frame_index * seg_frames + lax.broadcasted_iota(jnp.int32, mask_shape, 0) // per_frame
    )
    key_frame = lax.broadcasted_iota(jnp.int32, mask_shape, 1) // per_frame
    allowed = key_frame <= query_frame
    query_heads = lax.all_to_all(query_low, "row", split_axis=4, concat_axis=2, tiled=True)
    key_heads = lax.all_to_all(key_low, "row", split_axis=4, concat_axis=2, tiled=True)
    value_heads = lax.all_to_all(value_low, "row", split_axis=4, concat_axis=2, tiled=True)
    block_size = math.gcd(query_heads.shape[0], 4)

    def one_block(loop_carry, pieces):
        query_block, key_block, value_block = pieces
        keys_all, values_all = (
            lax.all_gather(key_block, "frame", axis=1, tiled=True),
            lax.all_gather(value_block, "frame", axis=1, tiled=True),
        )
        outputs = lax.map(
            partial(clip_forward, allowed, score_scale), (query_block, keys_all, values_all)
        )
        return (loop_carry, outputs)

    unused_carry, (attended_heads, log_total) = lax.scan(
        one_block,
        jnp.zeros((), jnp.float32),
        (
            block_split(query_heads, block_size),
            block_split(key_heads, block_size),
            block_split(value_heads, block_size),
        ),
    )
    attended_heads = block_join(attended_heads)
    log_total = block_join(log_total)
    attended_tok = lax.all_to_all(attended_heads, "row", split_axis=2, concat_axis=4, tiled=True)
    attended_tok, log_kept, query_kept, key_kept, value_kept = (
        attended_tok,
        log_total,
        query_heads,
        key_heads,
        value_heads,
    )
    attended_flat = attended_tok.reshape(token_count, model_width).astype(jnp.float32)
    gate_sig = jax.nn.sigmoid(gate_raw)
    gated_low = (attended_flat * gate_sig).astype(jnp.bfloat16)
    branch_one = jnp.dot(gated_low, full_out, preferred_element_type=jnp.float32).reshape(
        tokens.shape
    )
    after_one = token_f + gate_one * branch_one
    hidden_two, norm_two_pull = jax.vjp(modulate, after_one, shift_two, scale_two)
    hidden_two_low = hidden_two.astype(jnp.bfloat16).reshape(token_count, model_width)
    pre_act = jnp.dot(hidden_two_low, full_up, preferred_element_type=jnp.float32)
    act_values, gelu_pull = jax.vjp(partial(jax.nn.gelu, approximate=True), pre_act)
    act_low = act_values.astype(jnp.bfloat16)
    branch_two = contract_last(act_low, full_down).reshape(tokens.shape)
    mixed = (after_one + gate_two * branch_two).astype(jnp.bfloat16)
    full_in, full_out, full_up, full_down = (
        lax.all_gather(attn_in, "row", axis=0, tiled=True),
        lax.all_gather(out_weight, "row", axis=0, tiled=True),
        lax.all_gather(up_weight, "row", axis=0, tiled=True),
        lax.all_gather(down_weight, "row", axis=0, tiled=True),
    )
    grad_out = cotangent.astype(jnp.float32)
    grad_gate_two = jnp.sum(grad_out * branch_two, axis=(2, 3), keepdims=True)
    grad_branch_two = (grad_out * gate_two).astype(jnp.bfloat16).reshape(token_count, model_width)
    grad_act = jnp.dot(grad_branch_two, full_down, preferred_element_type=jnp.float32)
    (grad_pre,) = gelu_pull(grad_act)
    grad_pre_low = grad_pre.astype(jnp.bfloat16)
    grad_hidden_two = contract_last(grad_pre_low, full_up).reshape(tokens.shape)
    grad_after_part, grad_shift_two, grad_scale_two = norm_two_pull(grad_hidden_two)
    grad_after = grad_out + grad_after_part
    grad_gate_one = jnp.sum(grad_after * branch_one, axis=(2, 3), keepdims=True)
    grad_branch_one = (grad_after * gate_one).astype(jnp.bfloat16).reshape(token_count, model_width)
    grad_gated = contract_last(grad_branch_one, full_out)
    grad_attended = (grad_gated * gate_sig).astype(jnp.bfloat16).reshape(head_shape)
    grad_gate_raw = grad_gated * attended_flat * gate_sig * (1.0 - gate_sig)
    grad_heads = lax.all_to_all(grad_attended, "row", split_axis=4, concat_axis=2, tiled=True)
    block_size = math.gcd(clip_count, 4)

    def back_block(loop_carry, pieces):
        query_block, key_block, value_block, grad_block, log_block = pieces
        keys_all, values_all = (
            lax.all_gather(key_block, "frame", axis=1, tiled=True),
            lax.all_gather(value_block, "frame", axis=1, tiled=True),
        )
        grad_query, grad_key_all, grad_value_all = lax.map(
            partial(clip_backward, allowed, score_scale),
            (query_block, keys_all, values_all, grad_block, log_block),
        )
        grad_key, grad_value = (
            lax.psum_scatter(
                grad_key_all.astype(jnp.bfloat16), "frame", scatter_dimension=1, tiled=True
            ).astype(jnp.float32),
            lax.psum_scatter(
                grad_value_all.astype(jnp.bfloat16), "frame", scatter_dimension=1, tiled=True
            ).astype(jnp.float32),
        )
        return (loop_carry, (grad_query, grad_key, grad_value))

    unused_carry, (grad_query, grad_key, grad_value) = lax.scan(
        back_block,
        jnp.zeros((), jnp.float32),
        (
            block_split(query_kept, block_size),
            block_split(key_kept, block_size),
            block_split(value_kept, block_size),
            block_split(grad_heads, block_size),
            block_split(log_kept, block_size),
        ),
    )
    grad_query = block_join(grad_query).astype(jnp.bfloat16)
    grad_key = block_join(grad_key).astype(jnp.bfloat16)
    grad_value = block_join(grad_value).astype(jnp.bfloat16)
    query_back, key_back, value_back = (
        lax.all_to_all(grad_query, "row", split_axis=2, concat_axis=4, tiled=True),
        lax.all_to_all(grad_key, "row", split_axis=2, concat_axis=4, tiled=True),
        lax.all_to_all(grad_value, "row", split_axis=2, concat_axis=4, tiled=True),
    )
    query_unrot = rotate(
        query_back.reshape(token_count, HEADS, head_dim).astype(jnp.float32), cosines, -sines
    )
    key_unrot = rotate(
        key_back.reshape(token_count, HEADS, head_dim).astype(jnp.float32), cosines, -sines
    )
    grad_mixed_low = jnp.concatenate(
        [
            query_unrot.reshape(token_count, model_width),
            key_unrot.reshape(token_count, model_width),
            value_back.reshape(token_count, model_width).astype(jnp.float32),
            grad_gate_raw,
        ],
        axis=1,
    ).astype(jnp.bfloat16)
    grad_hidden_one = contract_last(grad_mixed_low, full_in).reshape(tokens.shape)
    grad_token_part, grad_shift_one, grad_scale_one = norm_one_pull(grad_hidden_one)
    tokens_grad = (grad_after + grad_token_part).astype(jnp.bfloat16)
    grad_mod_parts = jnp.stack(
        [
            grad_shift_one,
            grad_scale_one,
            grad_gate_one,
            grad_shift_two,
            grad_scale_two,
            grad_gate_two,
        ],
        axis=2,
    )
    grad_mod_parts = grad_mod_parts.reshape(clip_count, seg_frames, 6 * model_width)
    grad_mod_cols = lax.psum_scatter(
        grad_mod_parts.astype(jnp.bfloat16), "row", scatter_dimension=2, tiled=True
    )
    mod_weight_part = jnp.einsum(
        "cld,cle->de", silu_low, grad_mod_cols, preferred_element_type=jnp.float32
    )
    mod_bias_part = jnp.sum(grad_mod_cols.astype(jnp.float32), axis=(0, 1))
    grad_silu = jnp.einsum(
        "cle,de->cld", grad_mod_cols, mod_weight, preferred_element_type=jnp.float32
    )
    (grad_embedding,) = silu_pull(grad_silu)
    table_part = jnp.einsum(
        "cls,cld->sd", one_hot.astype(jnp.float32), grad_embedding, precision=lax.Precision.HIGHEST
    )
    grads_rows = lax.psum_scatter(
        jnp.concatenate(
            [
                contract_rows(hidden_low, grad_mixed_low),
                contract_rows(gated_low, grad_branch_one),
                contract_rows(hidden_two_low, grad_pre_low),
                contract_rows(grad_branch_two, act_low),
            ],
            axis=1,
        ).astype(jnp.bfloat16),
        "row",
        scatter_dimension=0,
        tiled=True,
    )
    summed_rows, mod_weight_grad, mod_bias_grad = (
        lax.psum(grads_rows, "frame").astype(jnp.float32),
        lax.psum(mod_weight_part.astype(jnp.bfloat16), "frame").astype(jnp.float32),
        lax.psum(mod_bias_part.astype(jnp.bfloat16), "frame").astype(jnp.float32),
    )
    noise_table_grad = lax.psum(table_part, ("frame", "row"))
    ff_width = full_up.shape[1]
    attn_in_grad = summed_rows[:, : 4 * model_width]
    out_weight_grad = summed_rows[:, 4 * model_width : 5 * model_width]
    up_weight_grad = summed_rows[:, 5 * model_width : 5 * model_width + ff_width]
    down_weight_grad = summed_rows[:, 5 * model_width + ff_width :]
    return (
        mixed,
        tokens_grad,
        noise_table_grad,
        mod_weight_grad,
        mod_bias_grad,
        attn_in_grad,
        out_weight_grad,
        up_weight_grad,
        down_weight_grad,
    )


def solution(mesh):
    in_specs = (
        P(None, "frame", "row", None, None),
        P(None, "frame"),
        P(),
        P(None, "row"),
        P("row"),
        P("row", None),
        P("row", None),
        P("row", None),
        P("row", None),
        P(None, "frame", "row", None, None),
    )
    out_specs = (
        P(None, "frame", "row", None, None),
        P(None, "frame", "row", None, None),
        P(),
        P(None, "row"),
        P("row"),
        P("row", None),
        P("row", None),
        P("row", None),
        P("row", None),
    )
    return jax.shard_map(
        on_device, mesh=mesh, in_specs=in_specs, out_specs=out_specs, check_vma=False
    )
```

profile of v0, /device:TPU:0, one launch (start us, length us, event | category | flops | bytes accessed | tf_op | source)
XLA Modules:
  0.0 1601.1 jit_solution(7836201947243075501)
XLA Ops:
  11.8 15.7 all-gather
  30.9 63.7 %all-gather.8.cloned.1.call-done = bf16[1024,4096]{1,0:T(8,128)(2,1)} async-done(((bf16[128,4096]{1,0:T(8,128)(2,1)}), bf16[1024,4096]{1,0:T(8,128)(2,1)}) %all-gather.8.cloned.1.call-update) | async-done | bytes 8388624 | tf_op jit(solution)/shard_map/all_gather | solution.py:184
  94.6 5.7 fusion.66
  108.4 17.7 %all_to_all.96 = bf16[8,2,16384]{2,1,0:T(2,128)(2,1)S(1)} all-to-all(bf16[8,2,16384]{2,1,0:T(2,128)(2,1)S(1)} %reshape.856), channel_id=1, replica_groups=mesh['frame'=4,'row'=8] {'row'}, dimensions={0} | all-to-all | bytes 1048576 | tf_op jit(solution)/shard_map/all_to_all | solution.py:221
  131.0 18.0 %all_to_all.97 = bf16[8,2,16384]{2,1,0:T(2,128)(2,1)S(1)} all-to-all(bf16[8,2,16384]{2,1,0:T(2,128)(2,1)S(1)} %reshape.852), channel_id=1, replica_groups=mesh['frame'=4,'row'=8] {'row'}, dimensions={0} | all-to-all | bytes 1048576 | tf_op jit(solution)/shard_map/all_to_all | solution.py:222
  160.4 13.4 add_compare_fusion
  179.6 55.4 %fusion = (f32[2,2048]{1,0:T(2,128)S(1)}, f32[2,2048,8192]{2,1,0:T(8,128)}) fusion(pred[2048,8192]{1,0:T(8,128)(4,1)} %add_compare_fusion, bf16[2,2048,64]{2,1,0:T(8,128)(2,1)S(1)} %bitcast.210, bf16[2,8192,64]{2,1,0:T(8,128)(2,1)} %bitcast.214), kind=kOutput, calls=%fused_computation.5 | convolution fusion | flops 4395626496 | bytes 153632768 | tf_op jit(solution)/shard_map/while/body/eval_jaxpr/while/body/eval_jaxpr/hqd,hkd->hqk/dot_general | solution.py:97
  235.1 47.5 %exponential_reduce_fusion = f32[2,2048]{1,0:T(2,128)S(1)} fusion(f32[2,2048,8192]{2,1,0:T(8,128)} %get-tuple-element.176, f32[2,2048]{1,0:T(2,128)S(1)} %is-finite_select_fusion, pred[2048,8192]{1,0:T(8,128)(4,1)} %add_compare_fusion), kind=kLoop, calls=%fused_computation.3 | loop fusion | flops 134213632 | bytes 151027712 | tf_op jit(solution)/shard_map/while/body/eval_jaxpr/while/body/eval_jaxpr/reduce_sum | solution.py:101
  282.7 52.9 %convolution_convert_fusion.4 = bf16[2,2048,64]{1,2,0:T(8,128)(2,1)S(1)} fusion(bf16[2,8192,64]{2,1,0:T(8,128)(2,1)} %bitcast.208, f32[2,2048,8192]{2,1,0:T(8,128)} %get-tuple-element.176, f32[2,2048]{1,0:T(2,128)S(1)} %log_add_fusion, pred[2048,8192]{1,0:T(8,128)(4,1)} %add_compare_fusion), kind=kOutput, calls=%fused_computation.27 | convolution fusion | flops 4429447168 | bytes 153632768 | tf_op jit(solution)/shard_map/while/body/eval_jaxpr/while/body/eval_jaxpr/hqk,hkd->hqd/dot_general | solution.py:103
  337.1 43.9 %all_to_all.98 = bf16[8,2,16384]{2,1,0:T(2,128)(2,1)S(1)} all-to-all(bf16[8,2,16384]{2,1,0:T(2,128)(2,1)S(1)} %reshape.858), channel_id=1, replica_groups=mesh['frame'=4,'row'=8] {'row'}, dimensions={0} | all-to-all | bytes 1048576 | tf_op jit(solution)/shard_map/all_to_all | solution.py:247
  395.1 8.2 fusion.67
  403.3 34.6 %all-gather.16.cloned.1.call-done = bf16[1024,4096]{1,0:T(8,128)(2,1)} async-done(((bf16[128,4096]{1,0:T(8,128)(2,1)}), bf16[1024,4096]{1,0:T(8,128)(2,1)}) %all-gather.16.cloned.1.call-update) | async-done | bytes 8388624 | tf_op jit(solution)/shard_map/all_gather | solution.py:186
  437.9 9.5 fusion.9
  447.5 8.0 fusion.68
  472.9 14.0 all-to-all-done.4
  487.7 102.5 %multiply_reduce_fusion = (f32[2,2048]{1,0:T(2,128)S(1)}, f32[2,2048,8192]{2,1,0:T(8,128)}) fusion(f32[2,2048,8192]{2,1,0:T(8,128)} %get-tuple-element.176, f32[2,2048]{1,0:T(2,128)S(1)} %log_add_fusion, pred[2048,8192]{1,0:T(8,128)(4,1)} %add_compare_fusion, bf16[2,2048,64]{2,1,0:T(8,128)(2,1)S(1)} %bitcast.212, bf16[2,8192,64]{2,1,0:T(8,128)(2,1)} %bitcast.209), kind=kOutput, calls=%fused_computation.1 | convolution fusion | flops 4462735360 | bytes 287866880 | tf_op jit(solution)/shard_map/while/body/eval_jaxpr/while/body/eval_jaxpr/hqd,hkd->hqk/dot_general | solution.py:123
  590.2 53.6 %convolution_convert_fusion = bf16[2,8192,64]{1,2,0:T(8,128)(2,1)} fusion(bf16[2,2048,64]{2,1,0:T(8,128)(2,1)S(1)} %bitcast.213, f32[2,2048,8192]{2,1,0:T(8,128)} %get-tuple-element.176, f32[2,2048]{1,0:T(2,128)S(1)} %log_add_fusion, pred[2048,8192]{1,0:T(8,128)(4,1)} %add_compare_fusion), kind=kOutput, calls=%fused_computation.11 | convolution fusion | flops 4430233600 | bytes 153632768 | tf_op jit(solution)/shard_map/while/body/eval_jaxpr/while/body/eval_jaxpr/hqk,hqd->hkd/dot_general | solution.py:122
  643.8 108.3 %multiply_convert_fusion = bf16[2,2048,8192]{2,1,0:T(8,128)(2,1)} fusion(f32[2,2048,8192]{2,1,0:T(8,128)} %get-tuple-element.183, f32[2,2048,8192]{2,1,0:T(8,128)} %get-tuple-element.176, f32[2,2048]{1,0:T(2,128)S(1)} %get-tuple-element.182, f32[2,2048]{1,0:T(2,128)S(1)} %log_add_fusion, pred[2048,8192]{1,0:T(8,128)(4,1)} %add_compare_fusion), kind=kLoop, calls=%fused_computation | loop fusion | flops 201326592 | bytes 352354304 | tf_op jit(solution)/shard_map/while/body/eval_jaxpr/while/body/eval_jaxpr/convert_element_type | solution.py:127
  752.1 24.3 %fusion.2 = bf16[2,8192,64]{1,2,0:T(8,128)(2,1)} fusion(bf16[2,2048,8192]{2,1,0:T(8,128)(2,1)} %multiply_convert_fusion, bf16[2,2048,64]{2,1,0:T(8,128)(2,1)S(1)} %bitcast.211), kind=kOutput, calls=%fused_computation.10 | convolution fusion | flops 4297064448 | bytes 69730304 | tf_op jit(solution)/shard_map/while/body/eval_jaxpr/while/body/eval_jaxpr/hqk,hqd->hkd/dot_general | solution.py:133
  786.1 29.8 %fusion.10 = bf16[2,2048,64]{1,2,0:T(8,128)(2,1)S(1)} fusion(bf16[2,2048,8192]{2,1,0:T(8,128)(2,1)} %multiply_convert_fusion, bf16[2,8192,64]{2,1,0:T(8,128)(2,1)} %bitcast.215), kind=kOutput, calls=%fused_computation.26 | convolution fusion | flops 4295491584 | bytes 69730304 | tf_op jit(solution)/shard_map/while/body/eval_jaxpr/while/body/eval_jaxpr/hqk,hkd->hqd/dot_general | solution.py:129
  821.8 8.0 convolution_convert_fusion.1
  829.8 127.1 %all-reduce.12.cloned.1.call-done = (bf16[1,32,16,16,2,64]{5,3,2,1,4,0:T(8,128)(2,1)}, bf16[1,32,16,16,2,64]{5,3,2,1,4,0:T(8,128)(2,1)}) async-done(((bf16[1,32,16,16,2,64]{5,3,2,1,4,0:T(8,128)(2,1)}, bf16[1,32,16,16,2,64]{5,3,2,1,4,0:T(8,128)(2,1)}), (bf16[1,32,16,16,2,64]{5,3,2,1,4,0:T(8,128)(2,1)}, bf16[1,32,16,16,2,64]{5,3,2,1,4,0:T(8,128)(2,1)})) %all-reduce.12.cloned.1.call-update) | async-done | bytes 4194320
  964.5 7.4 convolution_convert_fusion.2
  985.9 5.1 all-to-all-start.7
  1009.0 7.0 convolution_convert_fusion.3
  1016.1 5.9 fusion.29
  1025.7 18.8 %pad_maximum_fusion = bf16[1024,13312]{1,0:T(8,128)(2,1)} fusion(bf16[1024,4096]{1,0:T(8,128)(2,1)} %convolution_convert_fusion.1, bf16[1024,4096]{1,0:T(8,128)(2,1)} %convolution_convert_fusion.2, bf16[1024,1024]{1,0:T(8,128)(2,1)} %convolution_convert_fusion.5, bf16[1024,4096]{1,0:T(8,128)(2,1)} %convolution_convert_fusion.3), kind=kLoop, calls=%fused_computation.8 | loop fusion | flops 109051904 | bytes 54525952 | tf_op jit(solution)/shard_map/concatenate | solution.py:376
  1044.9 10.2 reduce-scatter.5.cloned.1.call-done
  1057.6 264.8 %reduce-scatter.7.cloned.1.call-done = bf16[128,13312]{1,0:T(8,128)(2,1)} async-done(((bf16[1024,13312]{1,0:T(8,128)(2,1)}), bf16[128,13312]{1,0:T(8,128)(2,1)}) %reduce-scatter.7.cloned.1.call-update) | async-done | bytes 3407888 | tf_op jit(solution)/shard_map/reduce_scatter | solution.py:375
  1326.9 10.3 psum.30
  1337.8 103.7 %all-reduce.10.cloned.1.call-done = (bf16[1024,768]{1,0:T(8,128)(2,1)}, bf16[128,13312]{1,0:T(8,128)(2,1)}) async-done(((bf16[1024,768]{1,0:T(8,128)(2,1)}, bf16[128,13312]{1,0:T(8,128)(2,1)}), (bf16[1024,768]{1,0:T(8,128)(2,1)}, bf16[128,13312]{1,0:T(8,128)(2,1)})) %all-reduce.10.cloned.1.call-update) | async-done | bytes 4980752 | tf_op jit(solution)/shard_map/psum | solution.py:391
  1448.7 140.7 %all-reduce.8.cloned.1.call-done = f32[1000,1024]{1,0:T(8,128)} async-done(((f32[1000,1024]{1,0:T(8,128)}), f32[1000,1024]{1,0:T(8,128)}) %all-reduce.8.cloned.1.call-update) | async-done | bytes 4096016 | tf_op jit(solution)/shard_map/psum | solution.py:394
  (289 shorter events, 148.9 us)
Async XLA Ops:
  7.2 21.8 %copy-start.56 = (f32[32]{0:T(128)S(1)}, f32[32]{0:T(128)}, u32[]{:S(2)}) copy-start(f32[32]{0:T(128)} %constant.181.clone) | copy-start | bytes 388
  7.2 21.8 %copy-start.57 = (f32[32]{0:T(128)S(1)}, f32[32]{0:T(128)}, u32[]{:S(2)}) copy-start(f32[32]{0:T(128)} %constant.182.clone) | copy-start | bytes 388
  7.2 21.8 %copy-start.58 = (f32[32]{0:T(128)S(1)}, f32[32]{0:T(128)}, u32[]{:S(2)}) copy-start(f32[32]{0:T(128)} %constant.183.clone) | copy-start | bytes 388
  7.2 87.4 %all-gather.8.cloned.1.call-start = ((), (), s32[]{:S(2)}) async-start(), calls=%async_computation.10 | async-start | bytes 9437184 | tf_op jit(solution)/shard_map/all_gather | solution.py:184
  8.0 171.6 %all-gather.10.cloned.1.call-start = ((), (), s32[]{:S(2)}) async-start(), calls=%async_computation.11 | async-start | bytes 5242880 | tf_op jit(solution)/shard_map/while/body/eval_jaxpr/all_gather | solution.py:228
  28.1 72.2 %copy-start.37 = (f32[8,2,16]{2,1,0:T(2,128)}, f32[8,2,16]{2,1,0:T(2,128)S(1)}, u32[]{:S(2)}) copy-start(f32[8,2,16]{2,1,0:T(2,128)S(1)} %broadcast_multiply_fusion.1) | copy-start | bytes 3076
  29.0 71.3 %copy-start.44 = (f32[8,2,16]{2,1,0:T(2,128)}, f32[8,2,16]{2,1,0:T(2,128)S(1)}, u32[]{:S(2)}) copy-start(f32[8,2,16]{2,1,0:T(2,128)S(1)} %fusion.53) | copy-start | bytes 3076
  29.9 74.7 %copy-start.39 = (f32[256,32]{0,1:T(8,128)}, f32[256,32]{0,1:T(8,128)S(1)}, u32[]{:S(2)}) copy-start(f32[256,32]{0,1:T(8,128)S(1)} %get-tuple-element.174) | copy-start | bytes 98308
  30.5 69.8 %copy-start.27 = (f32[8,1024]{1,0:T(8,128)}, f32[8,1024]{1,0:T(8,128)S(1)}, u32[]{:S(2)}) copy-start(f32[8,1024]{1,0:T(8,128)S(1)} %get-tuple-element.166) | copy-start | bytes 98308
  30.9 69.5 %copy-start.32 = (bf16[1,8,2,16,1024]{4,3,2,1,0:T(8,128)(2,1)}, bf16[1,8,2,16,1024]{4,3,2,1,0:T(8,128)(2,1)S(1)}, u32[]{:S(2)}) copy-start(bf16[1,8,2,16,1024]{4,3,2,1,0:T(8,128)(2,1)S(1)} %fusion.19) | copy-start | bytes 1572868
  128.0 154.6 %all-gather.12.cloned.1.call-start = ((), (), s32[]{:S(2)}) async-start(), calls=%async_computation.12 | async-start | bytes 5242880 | tf_op jit(solution)/shard_map/while/body/eval_jaxpr/all_gather | solution.py:229
  150.8 239.1 %all-gather.14.cloned.1.call-start = ((), (), s32[]{:S(2)}) async-start(), calls=%async_computation.13 | async-start | bytes 2359296 | tf_op jit(solution)/shard_map/all_gather | solution.py:185
  151.4 243.7 %all-gather.18.cloned.1.call-start = ((), (), s32[]{:S(2)}) async-start(), calls=%async_computation.15 | async-start | bytes 9437184 | tf_op jit(solution)/shard_map/all_gather | solution.py:187
  152.0 285.9 %all-gather.16.cloned.1.call-start = ((), (), s32[]{:S(2)}) async-start(), calls=%async_computation.14 | async-start | bytes 9437184 | tf_op jit(solution)/shard_map/all_gather | solution.py:186
  156.9 18.8 %all-to-all-start = ((bf16[8,2,16384]{2,1,0:T(2,128)(2,1)}), bf16[8,2,16384]{2,1,0:T(2,128)(2,1)S(1)}, u32[]{:S(2)}, u32[]{:S(2)}) async-start(bf16[8,2,16384]{2,1,0:T(2,128)(2,1)} %reshape.854), calls=%async_computation | async-start | bytes 1048576 | tf_op jit(solution)/shard_map/all_to_all | solution.py:220
  176.6 58.5 %copy-start.14 = (bf16[1,8,8,2,16,2,64]{6,4,3,2,1,5,0:T(8,128)(2,1)}, bf16[1,8,8,2,16,2,64]{6,4,3,2,1,5,0:T(8,128)(2,1)S(1)}, u32[]{:S(2)}) copy-start(bf16[1,8,8,2,16,2,64]{6,4,3,2,1,5,0:T(8,128)(2,1)S(1)} %copy.138) | copy-start | bytes 1572868
  395.1 42.8 %copy-start.25 = (bf16[1,8,2,16,1024]{4,3,2,1,0:T(8,128)(2,1)}, bf16[1,8,2,16,1024]{4,3,2,1,0:T(8,128)(2,1)S(1)}, u32[]{:S(2)}) copy-start(bf16[1,8,2,16,1024]{4,3,2,1,0:T(8,128)(2,1)S(1)} %get-tuple-element.185) | copy-start | bytes 1572868
  468.1 18.8 %all-to-all-start.4 = ((bf16[8,2,16384]{2,1,0:T(2,128)(2,1)}), bf16[8,2,16384]{2,1,0:T(2,128)(2,1)S(1)}, u32[]{:S(2)}, u32[]{:S(2)}) async-start(bf16[8,2,16384]{2,1,0:T(2,128)(2,1)} %reshape.860), calls=%async_computation.4 | async-start | bytes 1048576 | tf_op jit(solution)/shard_map/all_to_all | solution.py:289
  471.6 485.3 %all-reduce.12.cloned.1.call-start = ((), (), s32[]{:S(2)}) async-start(), calls=%async_computation.20 | async-start | bytes 16777216
  643.8 108.3 %copy-start.15 = (bf16[1,8,8,2,16,2,64]{6,4,3,2,1,5,0:T(8,128)(2,1)S(1)}, bf16[1,8,8,2,16,2,64]{6,4,3,2,1,5,0:T(8,128)(2,1)}, u32[]{:S(2)}) copy-start(bf16[1,8,8,2,16,2,64]{6,4,3,2,1,5,0:T(8,128)(2,1)} %copy-done.14) | copy-start | bytes 1572868
  818.2 141.7 %all-to-all-start.5 = ((bf16[8,2,16384]{2,1,0:T(2,128)(2,1)}), bf16[8,2,16384]{2,1,0:T(2,128)(2,1)S(1)}, u32[]{:S(2)}, u32[]{:S(2)}) async-start(bf16[8,2,16384]{2,1,0:T(2,128)(2,1)} %reshape.866), calls=%async_computation.5 | async-start | bytes 1048576 | tf_op jit(solution)/shard_map/all_to_all | solution.py:327
  829.8 134.8 %copy-start.26 = (bf16[1,8,2,16,1024]{4,3,2,1,0:T(8,128)(2,1)S(1)}, bf16[1,8,2,16,1024]{4,3,2,1,0:T(8,128)(2,1)}, u32[]{:S(2)}) copy-start(bf16[1,8,2,16,1024]{4,3,2,1,0:T(8,128)(2,1)} %copy-done.25) | copy-start | bytes 1572868
  959.9 25.2 %all-to-all-start.6 = ((bf16[8,2,16384]{2,1,0:T(2,128)(2,1)}), bf16[8,2,16384]{2,1,0:T(2,128)(2,1)S(1)}, u32[]{:S(2)}, u32[]{:S(2)}) async-start(bf16[8,2,16384]{2,1,0:T(2,128)(2,1)} %reshape.864), calls=%async_computation.6 | async-start | bytes 1048576 | tf_op jit(solution)/shard_map/all_to_all | solution.py:328
  985.9 20.4 %all-to-all-start.7 = ((bf16[8,2,16384]{2,1,0:T(2,128)(2,1)}), bf16[8,2,16384]{2,1,0:T(2,128)(2,1)S(1)}, u32[]{:S(2)}, u32[]{:S(2)}) async-start(bf16[8,2,16384]{2,1,0:T(2,128)(2,1)} %reshape.862), calls=%async_computation.7 | async-start | bytes 1048576 | tf_op jit(solution)/shard_map/all_to_all | solution.py:329
  991.0 64.1 %reduce-scatter.5.cloned.1.call-start = ((), (), s32[]{:S(2)}) async-start(), calls=%async_computation.16 | async-start | bytes 110592 | tf_op jit(solution)/shard_map/reduce_scatter | solution.py:361
  1025.6 296.8 %reduce-scatter.7.cloned.1.call-start = ((), (), s32[]{:S(2)}) async-start(), calls=%async_computation.18 | async-start | bytes 30670848 | tf_op jit(solution)/shard_map/reduce_scatter | solution.py:375
  1044.5 277.9 %copy-start.8 = (bf16[1024,768]{1,0:T(8,128)(2,1)S(1)}, bf16[1024,768]{1,0:T(8,128)(2,1)}, u32[]{:S(2)}) copy-start(bf16[1024,768]{1,0:T(8,128)(2,1)} %param.16) | copy-start | bytes 4718596
  1044.5 278.4 %copy-start.55 = (s32[1,8]{1,0:T(1,128)S(1)}, s32[1,8]{1,0:T(1,128)}, u32[]{:S(2)}) copy-start(s32[1,8]{1,0:T(1,128)} %param.14) | copy-start | bytes 100
  1044.6 397.0 %all-reduce.10.cloned.1.call-start = ((), (), s32[]{:S(2)}) async-start(), calls=%async_computation.19 | async-start | bytes 9961472 | tf_op jit(solution)/shard_map/psum | solution.py:391
  1055.0 267.4 %copy-start.48 = (bf16[1,8,768]{2,1,0:T(8,128)(2,1)S(1)}, bf16[1,8,768]{2,1,0:T(8,128)(2,1)}, u32[]{:S(2)}) copy-start(bf16[1,8,768]{2,1,0:T(8,128)(2,1)} %reduce-scatter.5.cloned.1.call-done) | copy-start | bytes 36868
  1322.4 267.0 %all-reduce.8.cloned.1.call-start = ((), (), s32[]{:S(2)}) async-start(), calls=%async_computation.17 | async-start | bytes 8192000 | tf_op jit(solution)/shard_map/psum | solution.py:394
  1445.8 148.3 %copy-start.1 = (bf16[1000,1024]{1,0:T(8,128)(2,1)S(1)}, bf16[1000,1024]{1,0:T(8,128)(2,1)}, u32[]{:S(2)}) copy-start(bf16[1000,1024]{1,0:T(8,128)(2,1)} %param.15) | copy-start | bytes 6144004
  (47 other events, 279.7 us)
Sparse Core Ops, SparseCore 0:
  9.6 84.9 all-gather.7
  128.1 51.4 all-gather.9
  182.0 52.5 all-gather.11
  236.1 29.1 all-gather.13
  266.7 81.4 all-gather.17
  349.6 88.2 all-gather.15
  786.2 170.6 all-reduce.11
  1025.7 29.2 reduce-scatter.4
  1057.4 264.9 reduce-scatter.6
  1326.4 115.0 all-reduce.9
  1447.6 141.7 all-reduce.7
where the time goes:
time: 1610 us; the launch traced here: 1600 us
  waiting for transfers between devices  769 us (48%)
  matrix products  402 us (25%)
  other arithmetic  205 us (13%)
  blocking collectives  106 us (7%)
  local copies, waits for them, and re-layouts  81.9 us (5%)
  starting transfers between devices  20.9 us (1%)
  between operations  16.3 us (1%)
    reduce_scatter x1, waiting for transfers between devices, on_device(): lax.psum_scatter(jnp.concatenate([contract_rows(hidden_low, grad_mixed_lo...  265 us
    psum x1, waiting for transfers between devices, on_device(): noise_table_grad = lax.psum(table_part, ('frame', 'row'))  141 us
    unnamed x12, waiting for transfers between devices  129 us
    convert_element_type x1, other arithmetic, clip_backward(): grad_scores = (prob_values * (grad_probs - row_inner)).astype(jnp.bfloat16)  108 us
    psum x1, waiting for transfers between devices, on_device(): lax.psum(mod_weight_part.astype(jnp.bfloat16), 'frame').astype(jnp.float32)  104 us
    dot_general x1, matrix products, clip_backward(): jnp.einsum('hqd,hkd->hqk', grad_head, value_head, preferred_element_type=...  102 us
    all_gather x1, waiting for transfers between devices, on_device(): lax.all_gather(attn_in, 'row', axis=0, tiled=True)  63.7 us
    dot_general x1, matrix products, clip_forward(): jnp.einsum('hqd,hkd->hqk', query_head, key_head, preferred_element_type=j...  55.4 us
  transfers between devices with their start and end apart: 16, of which 11 were waited for; matrix products, arithmetic and copies ran while one was open for 20% of the time, Pallas kernels for 0%

commit v1 on v0

v1 whole, which is shorter than its diff:
```python
from functools import partial

import jax
import jax.numpy as jnp
import numpy as np
from jax import lax
from jax.experimental import pallas as pl
from jax.experimental.pallas import tpu as pltpu
from jax.sharding import PartitionSpec as P

HEADS = 16
EPS = 1e-06
LOG2E = 1.4426950408889634
F32 = jnp.float32
BF = jnp.bfloat16
LANES = 128
MIB = 1 << 20


def rotary_freqs(pair_count):
    third_count = pair_count // 3
    group_sizes = [pair_count - 2 * third_count, third_count, third_count]
    tables = []
    offset = 0
    for group_index in range(3):
        freq_table = np.zeros((pair_count,), np.float32)
        for inner_index in range(group_sizes[group_index]):
            freq_table[offset + inner_index] = 10000.0 ** (-inner_index / group_sizes[group_index])
        offset += group_sizes[group_index]
        tables.append(freq_table)
    return tables


def layer_norm(values):
    row_mean = jnp.mean(values, axis=-1, keepdims=True)
    centered = values - row_mean
    row_var = jnp.mean(centered * centered, axis=-1, keepdims=True)
    return centered * lax.rsqrt(row_var + EPS)


def modulate(values, shift, scale_part):
    return layer_norm(values) * (1.0 + scale_part) + shift


def dot(left, right, left_dim, right_dim):
    return lax.dot_general(
        left, right, (((left_dim,), (right_dim,)), ((), ())), preferred_element_type=F32
    )


def swap_halves(values):
    lane = lax.broadcasted_iota(jnp.int32, values.shape, 1)
    width = values.shape[1]
    return jnp.where(
        (lane % 64) < 32, pltpu.roll(values, width - 32, 1), pltpu.roll(values, 32, 1)
    )


def low_lanes(shape):
    return lax.broadcasted_iota(jnp.int32, shape, len(shape) - 1) < 64


def qkv_kernel(heads, hid_ref, w_ref, cos_ref, sin_ref, pack_ref, gate_ref):
    clip, quarter = pl.program_id(0), pl.program_id(1)
    width = heads * 64
    mixed = jnp.dot(hid_ref[...], w_ref[...], preferred_element_type=F32)
    cos, sin = cos_ref[...], sin_ref[...]
    rows = mixed.shape[0]
    half = rows // 2
    gate_ref[...] = mixed[:, 3 * width :]
    low = low_lanes((rows, LANES))
    low_half = low_lanes((half, LANES))
    query_set = jnp.where((quarter == 0) | (quarter == 3), 0, 1)
    slot = quarter // 2
    for pair in range(heads // 2):
        cut = slice(pair * LANES, (pair + 1) * LANES)
        query = mixed[:, cut]
        key = mixed[:, width + pair * LANES : width + (pair + 1) * LANES]
        value = mixed[:, 2 * width + pair * LANES : 2 * width + (pair + 1) * LANES]
        query = query * cos + swap_halves(query) * sin
        key = key * cos + swap_halves(key) * sin
        key_turn = pltpu.roll(key, 64, 1)
        value_turn = pltpu.roll(value, 64, 1)
        query_turn = pltpu.roll(query, 64, 1)
        packs = (
            (
                jnp.where(low, key, value_turn),
                jnp.where(low_half, query[:half], query_turn[half:]),
            ),
            (
                jnp.where(low, key_turn, value),
                jnp.where(low_half, query_turn[:half], query[half:]),
            ),
        )
        for inner, (key_value, queries) in enumerate(packs):
            head = 2 * pair + inner
            pack_ref[clip, head, query_set, slot] = queries.astype(BF)
            key_value = key_value.astype(BF)
            first = 2 + 2 * (quarter % 2)
            pack_ref[clip, head, quarter // 2, first] = key_value[:half]
            pack_ref[clip, head, quarter // 2, first + 1] = key_value[half:]


def qkv_project(hidden, weight, cos, sin, clips, heads):
    tokens, width = hidden.shape
    quarter = tokens // clips // 4
    one = pl.Buffered(1)
    return pl.pallas_call(
        partial(qkv_kernel, heads),
        grid=(clips, 4),
        in_specs=[
            pl.BlockSpec((quarter, width), lambda c, i: (c * 4 + i, 0)),
            pl.BlockSpec(weight.shape, lambda c, i: (0, 0), pipeline_mode=one),
            pl.BlockSpec((quarter, LANES), lambda c, i: (i, 0)),
            pl.BlockSpec((quarter, LANES), lambda c, i: (i, 0)),
        ],
        out_specs=[
            pl.BlockSpec(
                (clips, heads, 2, 6, quarter // 2, LANES), lambda c, i: (0, 0, 0, 0, 0, 0)
            ),
            pl.BlockSpec((quarter, heads * 64), lambda c, i: (c * 4 + i, 0)),
        ],
        out_shape=[
            jax.ShapeDtypeStruct((clips, heads, 2, 6, quarter // 2, LANES), BF),
            jax.ShapeDtypeStruct((tokens, heads * 64), F32),
        ],
        compiler_params=pltpu.CompilerParams(
            dimension_semantics=("arbitrary", "arbitrary"), vmem_limit_bytes=48 * MIB
        ),
        name="qkv_project",
    )(hidden, weight, cos, sin)


def qkv_back_kernel(heads, pack_ref, dgate_ref, w_ref, cos_ref, sin_ref, mixed_ref, hid_ref):
    clip, quarter = pl.program_id(0), pl.program_id(1)
    width = heads * 64
    cos, sin = cos_ref[...], sin_ref[...]
    rows = cos.shape[0]
    half = rows // 2
    low_half = low_lanes((half, LANES))
    query_set = jnp.where((quarter == 0) | (quarter == 3), 0, 1)
    slot = quarter // 2
    first = 2 + 2 * (quarter % 2)
    low = low_lanes((rows, LANES))
    for pair in range(heads // 2):
        even, odd = 2 * pair, 2 * pair + 1
        query_even = pack_ref[clip, even, query_set, slot].astype(F32)
        query_odd = pack_ref[clip, odd, query_set, slot].astype(F32)
        query = jnp.concatenate(
            [
                jnp.where(low_half, query_even, pltpu.roll(query_odd, 64, 1)),
                jnp.where(low_half, pltpu.roll(query_even, 64, 1), query_odd),
            ],
            axis=0,
        )
        both = []
        for head in (even, odd):
            both.append(
                jnp.concatenate(
                    [
                        pack_ref[clip, head, quarter // 2, first].astype(F32),
                        pack_ref[clip, head, quarter // 2, first + 1].astype(F32),
                    ],
                    axis=0,
                )
            )
        key = jnp.where(low, both[0], pltpu.roll(both[1], 64, 1))
        value = jnp.where(low, pltpu.roll(both[0], 64, 1), both[1])
        query = query * cos - swap_halves(query) * sin
        key = key * cos - swap_halves(key) * sin
        for part, values in enumerate((query, key, value)):
            start = part * width + pair * LANES
            mixed_ref[:, start : start + LANES] = values.astype(BF)
    mixed_ref[:, 3 * width :] = dgate_ref[...]
    hid_ref[...] = dot(mixed_ref[...], w_ref[...], 1, 1).astype(BF)


def qkv_back(pack, dgate, weight, cos, sin, clips, heads):
    tokens = dgate.shape[0]
    width = weight.shape[0]
    quarter = tokens // clips // 4
    one = pl.Buffered(1)
    return pl.pallas_call(
        partial(qkv_back_kernel, heads),
        grid=(clips, 4),
        in_specs=[
            pl.BlockSpec(pack.shape, lambda c, i: (0, 0, 0, 0, 0, 0), pipeline_mode=one),
            pl.BlockSpec((quarter, heads * 64), lambda c, i: (c * 4 + i, 0)),
            pl.BlockSpec(weight.shape, lambda c, i: (0, 0), pipeline_mode=one),
            pl.BlockSpec((quarter, LANES), lambda c, i: (i, 0)),
            pl.BlockSpec((quarter, LANES), lambda c, i: (i, 0)),
        ],
        out_specs=[
            pl.BlockSpec((quarter, 4 * heads * 64), lambda c, i: (c * 4 + i, 0)),
            pl.BlockSpec((quarter, width), lambda c, i: (c * 4 + i, 0)),
        ],
        out_shape=[
            jax.ShapeDtypeStruct((tokens, 4 * heads * 64), BF),
            jax.ShapeDtypeStruct((tokens, width), BF),
        ],
        compiler_params=pltpu.CompilerParams(
            dimension_semantics=("arbitrary", "arbitrary"), vmem_limit_bytes=48 * MIB
        ),
        name="qkv_back",
    )(pack, dgate, weight, cos, sin)


def unpack_pair(even, odd):
    low = low_lanes(even.shape)
    return jnp.concatenate(
        [
            jnp.where(low, even, pltpu.roll(odd, 64, 1)),
            jnp.where(low, pltpu.roll(even, 64, 1), odd),
        ],
        axis=0,
    )


def gate_kernel(heads, pack_ref, gate_ref, gated_ref, attended_ref):
    clip, quarter = pl.program_id(0), pl.program_id(1)
    query_set = jnp.where((quarter == 0) | (quarter == 3), 0, 1)
    slot = quarter // 2
    for pair in range(heads // 2):
        cut = slice(pair * LANES, (pair + 1) * LANES)
        attended = unpack_pair(
            pack_ref[clip, 2 * pair, query_set, slot].astype(F32),
            pack_ref[clip, 2 * pair + 1, query_set, slot].astype(F32),
        )
        attended_ref[:, cut] = attended.astype(BF)
        gated_ref[:, cut] = (attended * jax.nn.sigmoid(gate_ref[:, cut])).astype(BF)


def gate_forward(pack, gate, clips, heads):
    tokens = gate.shape[0]
    quarter = tokens // clips // 4
    block = pl.BlockSpec((quarter, heads * 64), lambda c, i: (c * 4 + i, 0))
    return pl.pallas_call(
        partial(gate_kernel, heads),
        grid=(clips, 4),
        in_specs=[
            pl.BlockSpec(pack.shape, lambda c, i: (0, 0, 0, 0, 0, 0), pipeline_mode=pl.Buffered(1)),
            block,
        ],
        out_specs=[block, block],
        out_shape=[jax.ShapeDtypeStruct((tokens, heads * 64), BF)] * 2,
        compiler_params=pltpu.CompilerParams(dimension_semantics=("arbitrary", "arbitrary")),
        name="gate_forward",
    )(pack, gate)


def gate_back_kernel(heads, grad_ref, gate_ref, attended_ref, pack_ref, dgate_ref):
    clip, quarter = pl.program_id(0), pl.program_id(1)
    query_set = jnp.where((quarter == 0) | (quarter == 3), 0, 1)
    slot = quarter // 2
    rows = grad_ref.shape[0]
    half = rows // 2
    low = low_lanes((half, LANES))
    for pair in range(heads // 2):
        cut = slice(pair * LANES, (pair + 1) * LANES)
        sig = jax.nn.sigmoid(gate_ref[:, cut])
        grad = grad_ref[:, cut].astype(F32)
        dgate = grad * attended_ref[:, cut].astype(F32) * sig * (1.0 - sig)
        dgate_ref[:, cut] = dgate.astype(BF)
        down = grad * sig
        turn = pltpu.roll(down, 64, 1)
        pack_ref[clip, 2 * pair, query_set, slot] = jnp.where(low, down[:half], turn[half:]).astype(
            BF
        )
        pack_ref[clip, 2 * pair + 1, query_set, slot] = jnp.where(
            low, turn[:half], down[half:]
        ).astype(BF)


def gate_back(grad, gate, attended, clips, heads):
    tokens = gate.shape[0]
    quarter = tokens // clips // 4
    block = pl.BlockSpec((quarter, heads * 64), lambda c, i: (c * 4 + i, 0))
    pack_shape = (clips, heads, 2, 2, quarter // 2, LANES)
    return pl.pallas_call(
        partial(gate_back_kernel, heads),
        grid=(clips, 4),
        in_specs=[block, block, block],
        out_specs=[pl.BlockSpec(pack_shape, lambda c, i: (0, 0, 0, 0, 0, 0)), block],
        out_shape=[
            jax.ShapeDtypeStruct(pack_shape, BF),
            jax.ShapeDtypeStruct((tokens, heads * 64), BF),
        ],
        compiler_params=pltpu.CompilerParams(dimension_semantics=("arbitrary", "arbitrary")),
        name="gate_back",
    )(grad, gate, attended)


def tile_index(step):
    core = lax.axis_index("row") % 2
    slot = step // 2
    quarter = jnp.where(core == 0, 3 * slot, 1 + slot)
    return 2 * quarter + step % 2


def frame_mask(tile, per_frame):
    key = lax.broadcasted_iota(jnp.int32, (tile, 1), 0) // per_frame
    query = lax.broadcasted_iota(jnp.int32, (1, tile), 1) // per_frame
    return key <= query


def attend_kernel(tile, per_frame, scale, q_ref, kv_ref, out_ref, out_t_ref, lse_ref, vt_ref):
    step = pl.program_id(0)
    steps_of = scale * LOG2E

    @pl.when(step == 0)
    def _():
        vt_ref[64:72, :] = jnp.ones((8, vt_ref.shape[1]), BF)

        @pl.loop(0, kv_ref.shape[0] // tile)
        def _(j):
            rows = pl.ds(pl.multiple_of(j * tile, tile), tile)
            vt_ref[0:64, rows] = kv_ref[rows, :].T[64:, :]

    low = low_lanes((tile, LANES))
    packed = q_ref[...].astype(F32)
    packed = jnp.where(step % 2 == 0, packed, pltpu.roll(packed, 64, 1))
    query = jnp.where(low, packed, 0.0).astype(BF)

    def advance(j, carry, masked):
        top, total = carry
        rows = pl.ds(pl.multiple_of(j * tile, tile), tile)
        scores = dot(kv_ref[rows, :], query, 1, 1) * steps_of
        if masked:
            scores = jnp.where(frame_mask(tile, per_frame), scores, -1e30)
        new_top = jnp.maximum(top, jnp.max(scores, axis=0, keepdims=True))
        probs = jnp.exp2(scores - new_top).astype(BF)
        total = total * jnp.exp2(top - new_top) + dot(vt_ref[:, rows], probs, 1, 0)
        return new_top, total

    last = tile_index(step)
    carry = (jnp.full((1, tile), -1e30, F32), jnp.zeros((72, tile), F32))
    carry = lax.fori_loop(0, last, lambda j, c: advance(j, c, False), carry)
    top, total = advance(last, carry, True)
    norm = total[64:65, :]
    lse_ref[0] = top + jnp.log2(norm)
    result = (total[:64, :] / norm).astype(BF)

    @pl.when(step % 2 == 0)
    def _():
        out_t_ref[0, 0:64, :] = result

    @pl.when(step % 2 == 1)
    def _():
        out_t_ref[0, 64:128, :] = result
        out_ref[...] = out_t_ref[0].T


def attend(queries, keys_values, tile, per_frame, scale):
    one = pl.Buffered(1)
    return pl.pallas_call(
        partial(attend_kernel, tile, per_frame, scale),
        grid=(4,),
        in_specs=[
            pl.BlockSpec((tile, LANES), lambda i: (i // 2, 0)),
            pl.BlockSpec(keys_values.shape, lambda i: (0, 0), pipeline_mode=one),
        ],
        out_specs=[
            pl.BlockSpec((tile, LANES), lambda i: (i // 2, 0)),
            pl.BlockSpec((1, LANES, tile), lambda i: (i // 2, 0, 0)),
            pl.BlockSpec((1, 1, tile), lambda i: (i, 0, 0)),
        ],
        out_shape=[
            jax.ShapeDtypeStruct((2 * tile, LANES), BF),
            jax.ShapeDtypeStruct((2, LANES, tile), BF),
            jax.ShapeDtypeStruct((4, 1, tile), F32),
        ],
        scratch_shapes=[pltpu.VMEM((72, keys_values.shape[0]), BF)],
        compiler_params=pltpu.CompilerParams(
            dimension_semantics=("arbitrary",), vmem_limit_bytes=60 * MIB
        ),
        cost_estimate=pl.CostEstimate(
            flops=20_000_000_000, bytes_accessed=8_000_000, transcendentals=20_000_000
        ),
        name="attend",
    )(queries, keys_values)


def attend_back_kernel(
    tile,
    width,
    per_frame,
    scale,
    q_ref,
    do_ref,
    lse_ref,
    out_t_ref,
    kv_ref,
    dq_ref,
    dkv_ref,
    kt_ref,
    acc_ref,
    dq_t_ref,
    delta_ref,
):
    step = pl.program_id(0)
    steps_of = scale * LOG2E

    @pl.when(step == 0)
    def _():
        @pl.loop(0, kv_ref.shape[0] // tile)
        def _(j):
            rows = pl.ds(pl.multiple_of(j * tile, tile), tile)
            kt_ref[:, rows] = kv_ref[rows, :].T[:64, :]
            acc_ref[rows, :] = jnp.zeros((tile, LANES), F32)

    @pl.when(step % 2 == 0)
    def _():
        prod = do_ref[...].astype(F32).T * out_t_ref[0].astype(F32)
        delta_ref[0] = jnp.sum(prod[:64], axis=0, keepdims=True)
        delta_ref[1] = jnp.sum(prod[64:], axis=0, keepdims=True)

    low = low_lanes((tile, LANES))
    first = step % 2 == 0
    packed = q_ref[...].astype(F32)
    packed = jnp.where(first, packed, pltpu.roll(packed, 64, 1))
    query = jnp.where(low, packed, 0.0).astype(BF)
    packed = do_ref[...].astype(F32)
    packed = jnp.where(first, pltpu.roll(packed, 64, 1), packed)
    down = jnp.where(low, 0.0, packed).astype(BF)
    lse = lse_ref[0]
    delta = delta_ref[step % 2]

    def advance(j, dq, masked):
        rows = pl.ds(pl.multiple_of(j * width, width), width)
        pieces = kv_ref[rows, :]
        probs = jnp.exp2(dot(pieces, query, 1, 1) * steps_of - lse)
        if masked is not None:
            key = lax.broadcasted_iota(jnp.int32, (width, 1), 0) + masked
            ask = lax.broadcasted_iota(jnp.int32, (1, tile), 1)
            probs = jnp.where(key // per_frame <= ask // per_frame, probs, 0.0)
        dscore = (probs * (dot(pieces, down, 1, 1) - delta)).astype(BF)
        acc_ref[rows, :] += dot(dscore, query, 1, 0) + dot(probs.astype(BF), down, 1, 0)
        return dq + dot(kt_ref[:, rows], dscore, 1, 0)

    last = tile_index(step)
    parts = tile // width
    dq = jnp.zeros((64, tile), F32)
    dq = lax.fori_loop(0, last * parts, lambda j, c: advance(j, c, None), dq)
    for part in range(parts):
        dq = advance(last * parts + part, dq, part * width)
    dq = dq * scale

    @pl.when(step % 2 == 0)
    def _():
        dq_t_ref[0:64, :] = dq

    @pl.when(step % 2 == 1)
    def _():
        dq_t_ref[64:128, :] = dq
        dq_ref[...] = dq_t_ref[...].T.astype(BF)

    @pl.when(step == 3)
    def _():
        @pl.loop(0, kv_ref.shape[0] // tile)
        def _(j):
            rows = pl.ds(pl.multiple_of(j * tile, tile), tile)
            total = acc_ref[rows, :]
            dkv_ref[rows, :] = jnp.where(low_lanes((tile, LANES)), total * scale, total).astype(BF)


def attend_back(queries, downs, lse, out_t, keys_values, tile, per_frame, scale):
    one = pl.Buffered(1)
    keys = keys_values.shape[0]
    packed = pl.BlockSpec((tile, LANES), lambda i: (i // 2, 0))
    whole = pl.BlockSpec(keys_values.shape, lambda i: (0, 0), pipeline_mode=one)
    return pl.pallas_call(
        partial(attend_back_kernel, tile, tile // 2, per_frame, scale),
        grid=(4,),
        in_specs=[
            packed,
            packed,
            pl.BlockSpec((1, 1, tile), lambda i: (i, 0, 0)),
            pl.BlockSpec((1, LANES, tile), lambda i: (i // 2, 0, 0)),
            whole,
        ],
        out_specs=[packed, pl.BlockSpec(keys_values.shape, lambda i: (0, 0))],
        out_shape=[
            jax.ShapeDtypeStruct((2 * tile, LANES), BF),
            jax.ShapeDtypeStruct(keys_values.shape, BF),
        ],
        scratch_shapes=[
            pltpu.VMEM((64, keys), BF),
            pltpu.VMEM((keys, LANES), F32),
            pltpu.VMEM((LANES, tile), F32),
            pltpu.VMEM((2, 1, tile), F32),
        ],
        compiler_params=pltpu.CompilerParams(
            dimension_semantics=("arbitrary",), vmem_limit_bytes=60 * MIB
        ),
        cost_estimate=pl.CostEstimate(
            flops=50_000_000_000, bytes_accessed=12_000_000, transcendentals=20_000_000
        ),
        name="attend_back",
    )(queries, downs, lse, out_t, keys_values)


def on_device(
    tokens,
    timesteps,
    noise_table,
    mod_weight,
    mod_bias,
    attn_in,
    out_weight,
    up_weight,
    down_weight,
    cotangent,
):
    clips, frames, rows_dev, grid_side, width = tokens.shape
    frame_index = lax.axis_index("frame")
    row_index = lax.axis_index("row")
    frame_devs, row_devs = lax.axis_size("frame"), lax.axis_size("row")
    core = row_index % 2
    clip_len = frames * frame_devs
    head_dim = width // HEADS
    heads = HEADS // frame_devs
    slice_width = width // frame_devs
    per_frame_dev = rows_dev * grid_side
    per_frame = grid_side * grid_side
    token_count = clips * frames * per_frame_dev
    group_count = token_count * frame_devs
    tile = clip_len // 8 * per_frame
    scale = head_dim ** (-0.5)
    step_count = noise_table.shape[0]
    assert head_dim == 64 and row_devs == 2 * clips * heads

    def gather_frames(values):
        full = lax.all_gather(values, "frame", axis=1, tiled=True)
        return full.reshape(group_count, values.shape[-1])

    def scatter_frames(values):
        parts = values.reshape(clips, frame_devs, frames * per_frame_dev, width)
        parts = jnp.transpose(parts, (1, 0, 2, 3)).reshape(group_count, width)
        return lax.psum_scatter(parts, "frame", scatter_dimension=0, tiled=True).reshape(
            tokens.shape
        )

    def take_slice(weight, groups):
        cut = weight.reshape(weight.shape[0], groups, frame_devs, -1)
        cut = lax.dynamic_index_in_dim(cut, frame_index, 2, keepdims=False)
        return cut.reshape(weight.shape[0], -1)

    weight_in = lax.all_gather(take_slice(attn_in, 4), "row", axis=0, tiled=True)

    steps_iota = lax.broadcasted_iota(jnp.int32, (1, 1, step_count), 2)
    one_hot = (timesteps[:, :, None] == steps_iota).astype(BF)
    embedding = jnp.einsum("cls,sd->cld", one_hot, noise_table, preferred_element_type=F32)
    silu_low = jax.nn.silu(embedding).astype(BF)
    mod_local = jnp.einsum(
        "cld,de->cle", silu_low, mod_weight, preferred_element_type=F32
    ) + mod_bias.astype(F32)
    modulation = lax.all_gather(mod_local.astype(BF), "row", axis=2, tiled=True).astype(F32)
    modulation = modulation.reshape(clips, frames, 6, 1, 1, width)
    shift_one, scale_one, gate_one, shift_two, scale_two, gate_two = [
        modulation[:, :, part] for part in range(6)
    ]

    frame_freq, row_freq, col_freq = [np.tile(t, 4) for t in rotary_freqs(head_dim // 2)]
    shape_three = (clip_len, rows_dev, grid_side, LANES)
    frame_pos = lax.broadcasted_iota(F32, shape_three, 0)
    row_pos = (row_index * rows_dev + lax.broadcasted_iota(jnp.int32, shape_three, 1)).astype(F32)
    col_pos = lax.broadcasted_iota(F32, shape_three, 2)
    angles = (frame_pos * frame_freq + row_pos * row_freq + col_pos * col_freq).reshape(-1, LANES)
    sign = np.where(np.arange(LANES) % 64 < 32, -1.0, 1.0).astype(np.float32)
    cosines = jnp.cos(angles)
    sines = jnp.sin(angles) * sign

    token_f = tokens.astype(F32)
    hidden_one, norm_one_pull = jax.vjp(modulate, token_f, shift_one, scale_one)
    hidden_group = gather_frames(hidden_one.astype(BF))

    grad_out = cotangent.astype(F32)
    grad_branch_two = (grad_out * gate_two).astype(BF)

    pack, gate_raw = qkv_project(hidden_group, weight_in, cosines, sines, clips, heads)

    def exchange(values):
        return lax.all_to_all(values, "row", split_axis=0, concat_axis=0, tiled=True)

    half = tile // row_devs
    pairs = [(r, r ^ 1) for r in range(row_devs)]

    def to_heads(packed, count):
        parts = packed.reshape(row_devs, count, -1, per_frame_dev, LANES)
        return jnp.transpose(parts, (1, 2, 0, 3, 4)).reshape(-1, LANES)

    def to_tokens(values, count):
        parts = values.reshape(count, -1, row_devs, per_frame_dev, LANES)
        return jnp.transpose(parts, (2, 0, 1, 3, 4)).reshape(row_devs, count, half, LANES)

    arrived = exchange(pack.reshape(row_devs, 6, half, LANES))
    queries = to_heads(arrived[:, :2], 2)
    own_half = to_heads(arrived[:, 2:], 4)
    other_half = lax.ppermute(own_half, "row", pairs)
    keys_values = jnp.where(
        core == 0,
        jnp.concatenate([own_half, other_half], axis=0),
        jnp.concatenate([other_half, own_half], axis=0),
    )

    rest = jnp.concatenate([out_weight, take_slice(up_weight, 1), take_slice(down_weight, 1)], 1)
    rest = lax.all_gather(rest, "row", axis=0, tiled=True)
    full_out = rest[:, :width]
    weight_up = rest[:, width : width + up_weight.shape[1] // frame_devs]
    weight_down = rest[:, width + up_weight.shape[1] // frame_devs :]
    grad_two_group = gather_frames(grad_branch_two)

    attended_heads, attended_t, lse = attend(queries, keys_values, tile, per_frame, scale)
    pack_shape = (clips, heads, 2, 2, half, LANES)
    arrived = exchange(to_tokens(attended_heads, 2)).reshape(pack_shape)
    gated_group, attended = gate_forward(arrived, gate_raw, clips, heads)

    def group_split(values):
        parts = values.reshape(clips, frame_devs, frames * per_frame_dev, slice_width)
        parts = jnp.transpose(parts, (1, 0, 2, 3))
        return parts.reshape(frame_devs, token_count, slice_width)

    def group_join(values):
        parts = values.reshape(frame_devs, clips, frames * per_frame_dev, slice_width)
        return jnp.transpose(parts, (1, 0, 2, 3)).reshape(group_count, slice_width)

    gated = lax.all_to_all(group_split(gated_group), "frame", 0, 0, tiled=True)
    gated = jnp.transpose(gated, (1, 0, 2)).reshape(token_count, width)
    branch_one = jnp.dot(gated, full_out, preferred_element_type=F32).reshape(tokens.shape)
    after_one = token_f + gate_one * branch_one
    hidden_two, norm_two_pull = jax.vjp(modulate, after_one, shift_two, scale_two)
    hidden_two_group = gather_frames(hidden_two.astype(BF))

    pre_act = jnp.dot(hidden_two_group, weight_up, preferred_element_type=F32)
    act_values, gelu_pull = jax.vjp(partial(jax.nn.gelu, approximate=True), pre_act)
    act_low = act_values.astype(BF)
    grad_act = jnp.dot(grad_two_group, weight_down, preferred_element_type=F32)
    (grad_pre,) = gelu_pull(grad_act)
    grad_pre = grad_pre.astype(BF)
    grad_hidden_two = scatter_frames(dot(grad_pre, weight_up, 1, 1).astype(BF)).astype(F32)
    branch_two = scatter_frames(dot(act_low, weight_down, 1, 1).astype(BF)).astype(F32)
    mixed = (after_one + gate_two * branch_two).astype(BF)
    grad_gate_two = jnp.sum(grad_out * branch_two, axis=(2, 3), keepdims=True)

    grad_after_part, grad_shift_two, grad_scale_two = norm_two_pull(grad_hidden_two)
    grad_after = grad_out + grad_after_part
    grad_gate_one = jnp.sum(grad_after * branch_one, axis=(2, 3), keepdims=True)
    grad_branch_one = (grad_after * gate_one).astype(BF).reshape(token_count, width)
    grad_gated = dot(grad_branch_one, full_out, 1, 1).astype(BF)
    grad_gated = jnp.transpose(
        grad_gated.reshape(token_count, frame_devs, slice_width), (1, 0, 2)
    )
    grad_gated = group_join(lax.all_to_all(grad_gated, "frame", 0, 0, tiled=True))
    down_pack, grad_gate = gate_back(grad_gated, gate_raw, attended, clips, heads)
    downs = to_heads(exchange(down_pack.reshape(row_devs, 2, half, LANES)), 2)

    mlp_grads = jnp.concatenate(
        [
            dot(hidden_two_group, grad_pre, 0, 0),
            dot(grad_two_group, act_low, 0, 0),
            dot(gated, grad_branch_one, 0, 0),
        ],
        axis=1,
    ).astype(BF)
    mlp_grads = lax.psum_scatter(mlp_grads, "row", scatter_dimension=0, tiled=True)

    grad_queries, grad_kv = attend_back(
        queries, downs, lse, attended_t, keys_values, tile, per_frame, scale
    )
    grad_kv = grad_kv.reshape(2, -1, LANES)
    keep = lax.dynamic_index_in_dim(grad_kv, core, 0, keepdims=False)
    give = lax.dynamic_index_in_dim(grad_kv, 1 - core, 0, keepdims=False)
    got = lax.ppermute(give, "row", pairs)
    grad_kv = (keep.astype(F32) + got.astype(F32)).astype(BF)
    back_pack = jnp.concatenate([to_tokens(grad_queries, 2), to_tokens(grad_kv, 4)], axis=1)
    back_pack = exchange(back_pack).reshape(clips, heads, 2, 6, half, LANES)
    grad_mixed, grad_hidden = qkv_back(
        back_pack, grad_gate, weight_in, cosines, sines, clips, heads
    )
    grad_hidden_one = scatter_frames(grad_hidden).astype(F32)
    in_grad = lax.psum_scatter(
        dot(hidden_group, grad_mixed, 0, 0).astype(BF), "row", scatter_dimension=0, tiled=True
    )

    grad_token_part, grad_shift_one, grad_scale_one = norm_one_pull(grad_hidden_one)
    tokens_grad = (grad_after + grad_token_part).astype(BF)

    grad_mod = jnp.stack(
        [
            grad_shift_one,
            grad_scale_one,
            grad_gate_one,
            grad_shift_two,
            grad_scale_two,
            grad_gate_two,
        ],
        axis=2,
    ).reshape(clips * frames, 6 * width)
    grad_mod = lax.psum_scatter(grad_mod, "row", scatter_dimension=1, tiled=True).astype(BF)
    grad_mod_all = lax.all_gather(grad_mod, "frame", axis=0, tiled=True)
    steps_all = lax.all_gather(timesteps.reshape(-1), "frame", axis=0, tiled=True)
    hot_all = steps_all[:, None] == lax.broadcasted_iota(jnp.int32, (1, step_count), 1)
    embed_all = jnp.dot(hot_all.astype(BF), noise_table, preferred_element_type=F32)
    silu_all, silu_pull = jax.vjp(jax.nn.silu, embed_all)
    mod_weight_grad = dot(silu_all.astype(BF), grad_mod_all, 0, 0)
    mod_bias_grad = jnp.sum(grad_mod_all.astype(F32), axis=0)
    grad_silu = lax.psum(dot(grad_mod_all, mod_weight, 1, 1), "row")
    (grad_embedding,) = silu_pull(grad_silu)
    noise_table_grad = lax.dot_general(
        hot_all.astype(F32),
        grad_embedding,
        (((0,), (0,)), ((), ())),
        precision=lax.Precision.HIGHEST,
    )

    hidden_slice = up_weight.shape[1] // frame_devs
    up_part, down_part = mlp_grads[:, :hidden_slice], mlp_grads[:, hidden_slice : 2 * hidden_slice]
    out_weight_grad = lax.psum(mlp_grads[:, 2 * hidden_slice :], "frame").astype(F32)
    mlp_all = lax.all_gather(jnp.stack([up_part, down_part]), "frame", axis=0, tiled=False)

    def join_columns(parts):
        return jnp.transpose(parts, (1, 0, 2)).reshape(parts.shape[1], -1).astype(F32)

    up_weight_grad = join_columns(mlp_all[:, 0])
    down_weight_grad = join_columns(mlp_all[:, 1])
    in_all = lax.all_gather(in_grad, "frame", axis=0, tiled=False)
    in_all = in_all.reshape(frame_devs, in_grad.shape[0], 4, slice_width)
    attn_in_grad = jnp.transpose(in_all, (1, 2, 0, 3)).reshape(attn_in.shape).astype(F32)
    return (
        mixed,
        tokens_grad,
        noise_table_grad,
        mod_weight_grad,
        mod_bias_grad,
        attn_in_grad,
        out_weight_grad,
        up_weight_grad,
        down_weight_grad,
    )


def solution(mesh):
    in_specs = (
        P(None, "frame", "row", None, None),
        P(None, "frame"),
        P(),
        P(None, "row"),
        P("row"),
        P("row", None),
        P("row", None),
        P("row", None),
        P("row", None),
        P(None, "frame", "row", None, None),
    )
    out_specs = (
        P(None, "frame", "row", None, None),
        P(None, "frame", "row", None, None),
        P(),
        P(None, "row"),
        P("row"),
        P("row", None),
        P("row", None),
        P("row", None),
        P("row", None),
    )
    return jax.shard_map(
        on_device, mesh=mesh, in_specs=in_specs, out_specs=out_specs, check_vma=False
    )
```

time: 1610 us -> 952 us (0.59)
  matrix products: 402 us -> 59 us
  waiting for transfers between devices: 769 us -> 431 us
  other arithmetic: 205 us -> 49.6 us
  Pallas kernels: 0 us -> 110 us
  blocking collectives: 106 us -> 198 us
  local copies, waits for them, and re-layouts: 81.9 us -> 64.6 us
    dot_general x23 -> x15, matrix products: 402 us -> 59 us  [the longest x9 34.4 us: dot(): lax.dot_general(left, right, (((left_dim,), (right_dim,)), ((), ())), pre...]
    psum x2, waiting for transfers between devices: 244 us -> 66.8 us  [the longest x1 35.3 us: on_device(): lax.psum(mlp_grads[:, 2 * hidden_slice:], 'frame').astype(F32)]
    reduce_scatter x2 -> x5, waiting for transfers between devices: 275 us -> 103 us  [the longest x3 84 us: scatter_frames(): lax.psum_scatter(parts, 'frame', scatter_dimension=0, tiled=True)]
    pallas_call x0 -> x6, Pallas kernels: none -> 110 us  [the longest x1 58.4 us: attend_back(): pl.pallas_call(partial(attend_back_kernel, tile, tile // 2, per_frame, sc...]
    convert_element_type x11 -> x8, other arithmetic: 117 us -> 7.66 us  [the longest x1 1.96 us: on_device(): grad_branch_two = (grad_out * gate_two).astype(BF)]
    all_to_all x3 -> x5, blocking collectives: 79.6 us -> 166 us  [the longest x3 142 us: exchange(): lax.all_to_all(values, 'row', split_axis=0, concat_axis=0, tiled=True)]
    all_gather x6 -> x7, waiting for transfers between devices: 101 us -> 171 us  [the longest x3 81.9 us: gather_frames(): full = lax.all_gather(values, 'frame', axis=1, tiled=True)]
    unnamed x12 -> x16, waiting for transfers between devices: 129 us -> 71 us
  transfers between devices with their start and end apart: 16 -> 18, of which waited for: 11 -> 16; matrix products, arithmetic and copies ran while one was open for 20% -> 13% of each run, Pallas kernels for 0% -> 4%
where the time goes in v1:
time: 952 us; the launch traced here: 944 us
  waiting for transfers between devices  431 us (45%)
  blocking collectives  198 us (21%)
  Pallas kernels  110 us (12%)
  local copies, waits for them, and re-layouts  64.6 us (7%)
  matrix products  59 us (6%)
  other arithmetic  49.6 us (5%)
  starting transfers between devices  16.6 us (2%)
  between operations  15.7 us (2%)
    all_to_all x3, blocking collectives, exchange(): lax.all_to_all(values, 'row', split_axis=0, concat_axis=0, tiled=True)  142 us
    reduce_scatter x3, waiting for transfers between devices, scatter_frames(): lax.psum_scatter(parts, 'frame', scatter_dimension=0, tiled=True)  84 us
    all_gather x3, waiting for transfers between devices, gather_frames(): full = lax.all_gather(values, 'frame', axis=1, tiled=True)  81.9 us
    unnamed x16, waiting for transfers between devices  71 us
    pallas_call x1, Pallas kernels, attend_back(): pl.pallas_call(partial(attend_back_kernel, tile, tile // 2, per_frame, sc...  58.4 us
    psum x1, waiting for transfers between devices, on_device(): lax.psum(mlp_grads[:, 2 * hidden_slice:], 'frame').astype(F32)  35.3 us
    all_gather x1, waiting for transfers between devices, on_device(): lax.all_gather(jnp.stack([up_part, down_part]), 'frame', axis=0, tiled=Fa...  35 us
    dot_general x9, matrix products, dot(): lax.dot_general(left, right, (((left_dim,), (right_dim,)), ((), ())), pre...  34.4 us
  transfers between devices with their start and end apart: 18, of which 16 were waited for; matrix products, arithmetic and copies ran while one was open for 13% of the time, Pallas kernels for 4%

profile of v1, /device:TPU:0, one launch (start us, length us, event | category | flops | bytes accessed | tf_op | source)
XLA Modules:
  0.0 943.7 jit_solution(9120036640430299380)
XLA Ops:
  12.9 15.6 %all-gather = bf16[8,6144]{1,0:T(8,128)(2,1)S(1)} all-gather(bf16[8,768]{1,0:T(8,128)(2,1)S(1)} %fusion.35), channel_id=2, replica_groups=mesh['frame'=4,'row'=8] {'row'}, dimensions={1}, use_global_device_ids=true | all-gather | bytes 110592 | tf_op jit(solution)/shard_map/all_gather | solution.py:557
  46.1 20.1 %all-gather.12.cloned.1.call-done = bf16[1,32,2,16,1024]{4,3,2,0,1:T(8,128)(2,1)} async-done(((bf16[1,8,2,16,1024]{4,3,2,0,1:T(8,128)(2,1)}), bf16[1,32,2,16,1024]{4,3,2,0,1:T(8,128)(2,1)}) %all-gather.12.cloned.1.call-update) | async-done | bytes 2097168 | tf_op jit(solution)/shard_map/all_gather | solution.py:533
  66.1 31.4 %all-gather.14.cloned.1.call-done.w_ref = bf16[1024,1024]{1,0:T(8,128)(2,1)} async-done(((bf16[128,1024]{1,0:T(8,128)(2,1)}), bf16[1024,1024]{1,0:T(8,128)(2,1)}) %all-gather.14.cloned.1.call-update) | async-done | bytes 2097168 | tf_op jit(solution)/shard_map/all_gather | solution.py:548
  104.2 83.0 %all_to_all.30 = bf16[8,6,128,128]{3,2,1,0:T(8,128)(2,1)S(1)} all-to-all(bf16[8,6,128,128]{3,2,1,0:T(8,128)(2,1)S(1)} %bitcast.216), channel_id=1, replica_groups=mesh['frame'=4,'row'=8] {'row'}, dimensions={0} | all-to-all | bytes 3145728 | tf_op jit(solution)/shard_map/all_to_all | solution.py:583
  196.1 32.6 %attend.1 = (bf16[2048,128]{1,0:T(8,128)(2,1)}, bf16[2,128,1024]{2,1,0:T(8,128)(2,1)}, f32[4,1,1024]{2,1,0:T(1,128)}) custom-call(bf16[2048,128]{1,0:T(8,128)(2,1)} %bitcast.251, bf16[8192,128]{1,0:T(8,128)(2,1)} %maximum_select_fusion.kv_ref), custom_call_target="tpu_custom_call" | custom-call | flops 20000000000 | bytes 8000000 | tf_op jit(solution)/shard_map/attend/pallas_call | solution.py:355
  229.8 18.4 %all_to_all.31 = bf16[8,2,128,128]{3,2,1,0:T(8,128)(2,1)} all-to-all(bf16[8,2,128,128]{3,2,1,0:T(8,128)(2,1)S(1)} %bitcast.239), channel_id=1, replica_groups=mesh['frame'=4,'row'=8] {'row'}, dimensions={0} | all-to-all | bytes 1048576 | tf_op jit(solution)/shard_map/all_to_all | solution.py:583
  254.0 12.6 %all_to_all.32 = bf16[4,256,256]{1,2,0:T(8,128)(2,1)} all-to-all(bf16[4,256,256]{1,2,0:T(8,128)(2,1)} %copy.97), channel_id=1, replica_groups=mesh['frame'=4,'row'=8] {'frame'}, dimensions={0} | all-to-all | bytes 1048576 | tf_op jit(solution)/shard_map/all_to_all | solution.py:627
  274.7 30.9 %all-gather.18.cloned.1.call-done = bf16[1,32,2,16,1024]{4,3,2,0,1:T(8,128)(2,1)} async-done(((bf16[1,8,2,16,1024]{4,3,2,0,1:T(8,128)(2,1)}), bf16[1,32,2,16,1024]{4,3,2,0,1:T(8,128)(2,1)}) %all-gather.18.cloned.1.call-update) | async-done | bytes 2097168 | tf_op jit(solution)/shard_map/all_gather | solution.py:533
  305.6 6.6 fusion.14
  312.2 30.9 %all-gather.20.cloned.1.call-done = bf16[1,32,2,16,1024]{4,3,2,0,1:T(8,128)(2,1)} async-done(((bf16[1,8,2,16,1024]{4,3,2,0,1:T(8,128)(2,1)}), bf16[1,32,2,16,1024]{4,3,2,0,1:T(8,128)(2,1)}) %all-gather.20.cloned.1.call-update) | async-done | bytes 2097168 | tf_op jit(solution)/shard_map/all_gather | solution.py:533
  343.1 7.9 fusion.6
  357.6 10.9 %reduce-scatter.9.cloned.1.call-start = ((), (), s32[]{:S(2)}) async-start(), calls=%async_computation.16 | async-start | bytes 2621440 | tf_op jit(solution)/shard_map/reduce_scatter | solution.py:539
  368.5 7.1 convolution_convert_fusion.5
  375.6 17.3 %reduce-scatter.11.cloned.1.call-done = bf16[256,1024]{1,0:T(8,128)(2,1)} async-done(((bf16[1024,1024]{1,0:T(8,128)(2,1)}), bf16[256,1024]{1,0:T(8,128)(2,1)}) %reduce-scatter.11.cloned.1.call-update) | async-done | bytes 524304 | tf_op jit(solution)/shard_map/reduce_scatter | solution.py:539
  396.6 35.1 %reduce-scatter.9.cloned.1.call-done = bf16[256,1024]{1,0:T(8,128)(2,1)} async-done(((bf16[1024,1024]{1,0:T(8,128)(2,1)}), bf16[256,1024]{1,0:T(8,128)(2,1)}) %reduce-scatter.9.cloned.1.call-update) | async-done | bytes 524304 | tf_op jit(solution)/shard_map/reduce_scatter | solution.py:539
  438.0 11.7 %all_to_all.33 = bf16[4,256,256]{2,1,0:T(8,128)(2,1)} all-to-all(bf16[4,256,256]{2,1,0:T(8,128)(2,1)S(1)} %bitcast.240), channel_id=1, replica_groups=mesh['frame'=4,'row'=8] {'frame'}, dimensions={0} | all-to-all | bytes 1048576 | tf_op jit(solution)/shard_map/all_to_all | solution.py:653
  458.3 15.4 %all-to-all-done.4 = bf16[8,2,128,128]{3,2,1,0:T(8,128)(2,1)} async-done(((bf16[8,2,128,128]{3,2,1,0:T(8,128)(2,1)}), bf16[8,2,128,128]{3,2,1,0:T(8,128)(2,1)}, u32[]{:S(2)}, u32[]{:S(2)}) %all-to-all-start.4) | async-done | bytes 524320 | tf_op jit(solution)/shard_map/all_to_all | solution.py:583
  475.5 58.4 %attend_back.1 = (bf16[2048,128]{1,0:T(8,128)(2,1)}, bf16[8192,128]{1,0:T(8,128)(2,1)}) custom-call(bf16[2048,128]{1,0:T(8,128)(2,1)} %bitcast.252, bf16[2048,128]{1,0:T(8,128)(2,1)} %bitcast.255, f32[4,1,1024]{2,1,0:T(1,128)} %get-tuple-element.28.lse_ref, bf16[2,128,1024]{2,1,0:T(8,128)(2,1)} %get-tuple-element.29.out_t_ref, ...), custom_call_target="tpu_custom_call" | custom-call | flops 49999998976 | bytes 12000000 | tf_op jit(solution)/shard_map/attend_back/pallas_call | solution.py:471
  541.3 40.4 %all_to_all.34 = bf16[8,6,128,128]{3,2,1,0:T(8,128)(2,1)S(1)} all-to-all(bf16[8,6,128,128]{3,2,1,0:T(8,128)(2,1)S(1)} %pad_maximum_fusion.1), channel_id=1, replica_groups=mesh['frame'=4,'row'=8] {'row'}, dimensions={0} | all-to-all | bytes 3145728 | tf_op jit(solution)/shard_map/all_to_all | solution.py:583
  581.7 6.4 qkv_back.1
  590.6 31.6 %reduce-scatter.13.cloned.1.call-done = bf16[256,1024]{1,0:T(8,128)(2,1)} async-done(((bf16[1024,1024]{1,0:T(8,128)(2,1)}), bf16[256,1024]{1,0:T(8,128)(2,1)}) %reduce-scatter.13.cloned.1.call-update) | async-done | bytes 524304 | tf_op jit(solution)/shard_map/reduce_scatter | solution.py:539
  627.0 5.9 convolution_convert_fusion.3
  641.6 13.2 %pad_maximum_fusion = bf16[1024,3072]{0,1:T(8,128)(2,1)} fusion(bf16[1024,1024]{0,1:T(8,128)(2,1)S(1)} %convolution_convert_fusion, bf16[1024,1024]{0,1:T(8,128)(2,1)S(1)} %convolution_convert_fusion.1, bf16[1024,1024]{0,1:T(8,128)(2,1)S(1)} %convolution_convert_fusion.2), kind=kLoop, calls=%fused_computation | loop fusion | flops 18874368 | bytes 12582912 | tf_op jit(solution)/shard_map/concatenate | solution.py:657
  654.9 8.7 copy.122
  664.4 8.2 all_gather.43
  675.3 19.3 %reduce-scatter.17.cloned.1.call-done = bf16[128,1024]{1,0:T(8,128)(2,1)} async-done(((bf16[1024,1024]{1,0:T(8,128)(2,1)}), bf16[128,1024]{1,0:T(8,128)(2,1)}) %reduce-scatter.17.cloned.1.call-update) | async-done | bytes 262160 | tf_op jit(solution)/shard_map/reduce_scatter | solution.py:681
  694.7 70.7 %reduce-scatter.19.cloned.1.call-done = bf16[128,3072]{1,0:T(8,128)(2,1)} async-done(((bf16[1024,3072]{1,0:T(8,128)(2,1)}), bf16[128,3072]{1,0:T(8,128)(2,1)}) %reduce-scatter.19.cloned.1.call-update) | async-done | bytes 786448
  777.2 7.5 all-reduce
  790.1 31.5 %all-reduce.4.cloned.1.call-done = f32[32,1024]{1,0:T(8,128)} async-done(((f32[32,1024]{1,0:T(8,128)}), f32[32,1024]{1,0:T(8,128)}) %all-reduce.4.cloned.1.call-update) | async-done | bytes 131088 | tf_op jit(solution)/shard_map/psum | solution.py:707
  826.4 22.7 %all-gather.22.cloned.1.call-done = bf16[512,1024]{1,0:T(8,128)(2,1)} async-done(((bf16[128,1024]{1,0:T(8,128)(2,1)}), bf16[512,1024]{1,0:T(8,128)(2,1)}) %all-gather.22.cloned.1.call-update) | async-done | bytes 1048592 | tf_op jit(solution)/shard_map/all_gather | solution.py:726
  859.6 35.3 %all-reduce.6.cloned.1.call-done = bf16[128,1024]{0,1:T(8,128)(2,1)} async-done(((bf16[128,1024]{0,1:T(8,128)(2,1)}), bf16[128,1024]{0,1:T(8,128)(2,1)}) %all-reduce.6.cloned.1.call-update) | async-done | bytes 262160 | tf_op jit(solution)/shard_map/psum | solution.py:718
  896.8 35.0 %all-gather.24.cloned.1.call-done = bf16[8,128,1024]{2,1,0:T(8,128)(2,1)} async-done(((bf16[2,128,1024]{2,1,0:T(8,128)(2,1)}), bf16[8,128,1024]{2,1,0:T(8,128)(2,1)}) %all-gather.24.cloned.1.call-update) | async-done | bytes 2097168 | tf_op jit(solution)/shard_map/all_gather | solution.py:719
  (194 shorter events, 145.6 us)
Async XLA Ops:
  7.2 58.9 %all-gather.12.cloned.1.call-start = ((), (), s32[]{:S(2)}) async-start(), calls=%async_computation.12 | async-start | bytes 2621440 | tf_op jit(solution)/shard_map/all_gather | solution.py:533
  10.6 17.9 %copy-start.22 = (f32[8,2,16]{2,1,0:T(2,128)}, f32[8,2,16]{2,1,0:T(2,128)S(1)}, u32[]{:S(2)}) copy-start(f32[8,2,16]{2,1,0:T(2,128)S(1)} %fusion.43) | copy-start | bytes 3076
  10.6 17.9 %copy-start.7 = (bf16[1,8,2,16,1024]{4,3,2,1,0:T(8,128)(2,1)S(1)}, bf16[1,8,2,16,1024]{4,3,2,1,0:T(8,128)(2,1)}, u32[]{:S(2)}) copy-start(bf16[1,8,2,16,1024]{4,3,2,1,0:T(8,128)(2,1)} %param.14) | copy-start | bytes 1572868
  29.8 67.7 %all-gather.14.cloned.1.call-start = ((), (), s32[]{:S(2)}) async-start(), calls=%async_computation.13 | async-start | bytes 2359296 | tf_op jit(solution)/shard_map/all_gather | solution.py:548
  34.1 232.6 %all-gather.16.cloned.1.call-start = ((), (), s32[]{:S(2)}) async-start(), calls=%async_computation.14 | async-start | bytes 7077888 | tf_op jit(solution)/shard_map/all_gather | solution.py:607
  38.0 5.4 copy-start.25
  42.9 262.7 %all-gather.18.cloned.1.call-start = ((), (), s32[]{:S(2)}) async-start(), calls=%async_computation.15 | async-start | bytes 2621440 | tf_op jit(solution)/shard_map/all_gather | solution.py:533
  104.1 83.1 %copy-start.1 = (f32[1024,256]{1,0:T(8,128)}, f32[1024,256]{1,0:T(8,128)S(1)}, u32[]{:S(2)}) copy-start(f32[1024,256]{1,0:T(8,128)S(1)} %get-tuple-element.24.gate_ref) | copy-start | bytes 3145732
  188.7 3.3 collective-permute-start
  272.3 70.8 %all-gather.20.cloned.1.call-start = ((), (), s32[]{:S(2)}) async-start(), calls=%async_computation.17 | async-start | bytes 2621440 | tf_op jit(solution)/shard_map/all_gather | solution.py:533
  274.3 118.6 %reduce-scatter.11.cloned.1.call-start = ((), (), s32[]{:S(2)}) async-start(), calls=%async_computation.18 | async-start | bytes 2621440 | tf_op jit(solution)/shard_map/reduce_scatter | solution.py:539
  357.6 74.1 %reduce-scatter.9.cloned.1.call-start = ((), (), s32[]{:S(2)}) async-start(), calls=%async_computation.16 | async-start | bytes 2621440 | tf_op jit(solution)/shard_map/reduce_scatter | solution.py:539
  453.6 20.0 %all-to-all-start.4 = ((bf16[8,2,128,128]{3,2,1,0:T(8,128)(2,1)}), bf16[8,2,128,128]{3,2,1,0:T(8,128)(2,1)}, u32[]{:S(2)}, u32[]{:S(2)}) async-start(bf16[8,2,128,128]{3,2,1,0:T(8,128)(2,1)} %bitcast.253), calls=%async_computation.6 | async-start | bytes 1048576 | tf_op jit(solution)/shard_map/all_to_all | solution.py:583
  458.2 164.0 %reduce-scatter.13.cloned.1.call-start = ((), (), s32[]{:S(2)}) async-start(), calls=%async_computation.19 | async-start | bytes 2621440 | tf_op jit(solution)/shard_map/reduce_scatter | solution.py:539
  536.2 3.0 collective-permute-start.1
  541.3 40.4 %copy-start.3 = (bf16[1024,256]{1,0:T(8,128)(2,1)S(1)}, bf16[1024,256]{1,0:T(8,128)(2,1)}, u32[]{:S(2)}) copy-start(bf16[1024,256]{1,0:T(8,128)(2,1)} %get-tuple-element.32.dgate_ref) | copy-start | bytes 1572868
  589.4 32.8 %copy-start.9 = (bf16[1,8,2,16,1024]{4,3,2,1,0:T(8,128)(2,1)S(1)}, bf16[1,8,2,16,1024]{4,3,2,1,0:T(8,128)(2,1)}, u32[]{:S(2)}) copy-start(bf16[1,8,2,16,1024]{4,3,2,1,0:T(8,128)(2,1)} %param.14) | copy-start | bytes 1572868
  589.4 35.4 %copy-start.23 = (f32[8,2,16]{2,1,0:T(2,128)S(1)}, f32[8,2,16]{2,1,0:T(2,128)}, u32[]{:S(2)}) copy-start(f32[8,2,16]{2,1,0:T(2,128)} %copy-done.22) | copy-start | bytes 3076
  589.4 74.2 %reduce-scatter.15.cloned.1.call-start = ((), (), s32[]{:S(2)}) async-start(), calls=%async_computation.20 | async-start | bytes 221184 | tf_op jit(solution)/shard_map/reduce_scatter | solution.py:699
  624.9 8.0 copy-start.20
  626.9 67.7 %reduce-scatter.17.cloned.1.call-start = ((), (), s32[]{:S(2)}) async-start(), calls=%async_computation.22 | async-start | bytes 2359296 | tf_op jit(solution)/shard_map/reduce_scatter | solution.py:681
  632.9 132.5 %reduce-scatter.19.cloned.1.call-start = ((), (), s32[]{:S(2)}) async-start(), calls=%async_computation.26 | async-start | bytes 7077888
  633.2 4.8 copy-start.27
  633.2 4.8 copy-start.29
  663.6 158.1 %all-reduce.4.cloned.1.call-start = ((), (), s32[]{:S(2)}) async-start(), calls=%async_computation.21 | async-start | bytes 262144 | tf_op jit(solution)/shard_map/psum | solution.py:707
  675.2 173.8 %all-gather.22.cloned.1.call-start = ((), (), s32[]{:S(2)}) async-start(), calls=%async_computation.24 | async-start | bytes 1310720 | tf_op jit(solution)/shard_map/all_gather | solution.py:726
  694.6 200.3 %all-reduce.6.cloned.1.call-start = ((), (), s32[]{:S(2)}) async-start(), calls=%async_computation.23 | async-start | bytes 524288 | tf_op jit(solution)/shard_map/psum | solution.py:718
  769.1 6.7 copy-start.28
  769.1 7.9 copy-start.26
  769.2 162.6 %all-gather.24.cloned.1.call-start = ((), (), s32[]{:S(2)}) async-start(), calls=%async_computation.25 | async-start | bytes 2621440 | tf_op jit(solution)/shard_map/all_gather | solution.py:719
  773.7 11.6 %copy-start.24 = (f32[8,2,16]{2,1,0:T(2,128)S(1)}, f32[8,2,16]{2,1,0:T(2,128)}, u32[]{:S(2)}) copy-start(f32[8,2,16]{2,1,0:T(2,128)} %get-tuple-element.83) | copy-start | bytes 3076
  773.7 11.6 %copy-start.21 = (f32[8,2,16]{2,1,0:T(2,128)S(1)}, f32[8,2,16]{2,1,0:T(2,128)}, u32[]{:S(2)}) copy-start(f32[8,2,16]{2,1,0:T(2,128)} %copy-done.20) | copy-start | bytes 3076
  (17 other events, 32.6 us)
Sparse Core Ops, SparseCore 0:
  29.9 36.1 all-gather.11
  68.3 29.1 all-gather.13
  99.7 97.2 all-gather.15
  272.4 33.1 all-gather.17
  307.9 35.1 all-gather.19
  357.7 35.1 reduce-scatter.10
  396.5 35.1 reduce-scatter.8
  589.6 32.5 reduce-scatter.12
  627.0 30.6 reduce-scatter.14
  660.5 34.0 reduce-scatter.16
  696.9 68.4 reduce-scatter.18
  768.1 53.4 all-reduce.3
  823.5 25.5 all-gather.21
  851.8 43.0 all-reduce.5
  896.6 35.1 all-gather.23

commit v2 on v1

--- a/solution.py
+++ b/solution.py
@@ -499,6 +499,185 @@
     )(queries, downs, lse, out_t, keys_values)
 
 
+def exchange_kernel(axis, moves, sources, results, pair_of, finish, *refs):
+    in_refs, refs = refs[:sources], refs[sources:]
+    out_refs, refs = refs[:results], refs[results:]
+    send_sem, recv_sem, own_sem = refs[-3:]
+    scratch = refs[:-3]
+    dests = scratch if finish is not None else out_refs
+    me, count = lax.axis_index(axis), lax.axis_size(axis)
+    barrier = pltpu.get_barrier_semaphore()
+    for step in range(1, count):
+        pl.semaphore_signal(
+            barrier,
+            inc=1,
+            device_id={axis: lax.rem(me + step, count)},
+            device_id_type=pl.DeviceIdType.MESH,
+        )
+    pl.semaphore_wait(barrier, count - 1)
+    copies = []
+    for step in range(1, count):
+        peer = lax.rem(me + step, count)
+        for index, (source, dest, take, place) in enumerate(moves):
+            copies.append(
+                pltpu.make_async_remote_copy(
+                    src_ref=take(in_refs[source], peer),
+                    dst_ref=place(dests[dest], me, peer),
+                    send_sem=send_sem.at[index, step - 1],
+                    recv_sem=recv_sem.at[index, step - 1],
+                    device_id={axis: peer},
+                    device_id_type=pl.DeviceIdType.MESH,
+                )
+            )
+            copies[-1].start()
+    for index, (source, dest, take, place) in enumerate(moves):
+        copies.append(
+            pltpu.make_async_copy(
+                take(in_refs[source], me), place(dests[dest], me, me), own_sem.at[index]
+            )
+        )
+        copies[-1].start()
+    for copy in copies:
+        copy.wait()
+    if pair_of is not None:
+        core = lax.rem(me, 2)
+        ref = dests[pair_of].at[core]
+        copy = pltpu.make_async_remote_copy(
+            src_ref=ref,
+            dst_ref=ref,
+            send_sem=own_sem.at[len(moves)],
+            recv_sem=own_sem.at[len(moves) + 1],
+            device_id={axis: me + 1 - 2 * core},
+            device_id_type=pl.DeviceIdType.MESH,
+        )
+        copy.start()
+        copy.wait()
+    if finish is not None:
+        finish(dests, out_refs)
+
+
+def exchange(name, axis, number, moves, arrays, shapes, pair_of=None, finish=None, landing=()):
+    count = lax.axis_size(axis)
+    vmem = pl.BlockSpec(memory_space=pltpu.VMEM)
+    sent = sum(a.size * a.dtype.itemsize for a in arrays)
+    return pl.pallas_call(
+        partial(exchange_kernel, axis, moves, len(arrays), len(shapes), pair_of, finish),
+        in_specs=[vmem] * len(arrays),
+        out_specs=[vmem] * len(shapes),
+        out_shape=[jax.ShapeDtypeStruct(*shape) for shape in shapes],
+        scratch_shapes=[pltpu.VMEM(*shape) for shape in landing]
+        + [
+            pltpu.SemaphoreType.DMA((len(moves), count - 1)),
+            pltpu.SemaphoreType.DMA((len(moves), count - 1)),
+            pltpu.SemaphoreType.DMA((len(moves) + 2,)),
+        ],
+        compiler_params=pltpu.CompilerParams(
+            collective_id=number, has_side_effects=True, vmem_limit_bytes=40 * MIB
+        ),
+        cost_estimate=pl.CostEstimate(
+            flops=0, bytes_accessed=20_000_000 + 30 * sent, transcendentals=0
+        ),
+        name=name,
+    )(*arrays)
+
+
+def all_of(ref, peer):
+    return ref
+
+
+def block_of(ref, peer):
+    return ref.at[peer]
+
+
+def at_sender(ref, me, peer):
+    return ref.at[me]
+
+
+def lanes_of(size):
+    def view(ref, peer):
+        return ref.at[:, pl.ds(pl.multiple_of(peer * size, LANES), size)]
+
+    return view
+
+
+def lanes_at(size):
+    def view(ref, me, peer):
+        return ref.at[:, pl.ds(pl.multiple_of(me * size, LANES), size)]
+
+    return view
+
+
+def add_landed(dests, out_refs):
+    landed, out = dests[0], out_refs[0]
+    rows = out.shape[0]
+    step = 32 if rows % 32 == 0 else rows
+
+    @pl.loop(0, rows // step)
+    def _(j):
+        cut = pl.ds(pl.multiple_of(j * step, step), step)
+        total = landed[0, cut, :].astype(F32)
+        for other in range(1, landed.shape[0]):
+            total += landed[other, cut, :].astype(F32)
+        out[cut, :] = total.astype(out.dtype)
+
+
+def gather(name, axis, number, arrays):
+    count = lax.axis_size(axis)
+    moves = [(i, i, all_of, at_sender) for i in range(len(arrays))]
+    return exchange(
+        name, axis, number, moves, arrays, [((count,) + a.shape, a.dtype) for a in arrays]
+    )
+
+
+def scatter_sum(name, axis, number, parts, dtype=F32):
+    return exchange(
+        name,
+        axis,
+        number,
+        [(0, 0, block_of, at_sender)],
+        [parts],
+        [(parts.shape[1:], dtype)],
+        finish=add_landed,
+        landing=[(parts.shape, parts.dtype)],
+    )[0]
+
+
+def mlp_grads_kernel(cut, *refs):
+    out_ref = refs[-1]
+    start = 0
+    for part in range(len(refs) // 2):
+        left, right = refs[2 * part], refs[2 * part + 1]
+        columns = right.shape[1]
+        result = dot(left[...], right[...], 0, 0).astype(BF)
+        for block in range(out_ref.shape[0]):
+            out_ref[block, :, start : start + columns] = result[block * cut : (block + 1) * cut]
+        start += columns
+
+
+def mlp_grads(pairs, row_devs):
+    cut = pairs[0][0].shape[1] // row_devs
+    block = max(cut, LANES)
+    in_specs = []
+    for left, right in pairs:
+        in_specs.append(pl.BlockSpec((left.shape[0], block), lambda i: (0, i)))
+        in_specs.append(pl.BlockSpec(right.shape, lambda i: (0, 0), pipeline_mode=pl.Buffered(1)))
+    columns = sum(right.shape[1] for _, right in pairs)
+    return pl.pallas_call(
+        partial(mlp_grads_kernel, cut),
+        grid=(row_devs * cut // block,),
+        in_specs=in_specs,
+        out_specs=pl.BlockSpec((block // cut, cut, columns), lambda i: (i, 0, 0)),
+        out_shape=jax.ShapeDtypeStruct((row_devs, cut, columns), BF),
+        compiler_params=pltpu.CompilerParams(
+            dimension_semantics=("arbitrary",), vmem_limit_bytes=48 * MIB
+        ),
+        cost_estimate=pl.CostEstimate(
+            flops=5_000_000_000, bytes_accessed=18_000_000, transcendentals=0
+        ),
+        name="mlp_grads",
+    )(*[array for pair in pairs for array in pair])
+
+
 def on_device(
     tokens,
     timesteps,
@@ -529,13 +708,20 @@
     step_count = noise_table.shape[0]
     assert head_dim == 64 and row_devs == 2 * clips * heads
 
+    def by_frames(values):
+        parts = values.reshape(frame_devs, clips, frames * per_frame_dev, -1)
+        return jnp.transpose(parts, (1, 0, 2, 3)).reshape(group_count, values.shape[-1])
+
+    def to_frames(values):
+        parts = values.reshape(clips, frame_devs, frames * per_frame_dev, -1)
+        return jnp.transpose(parts, (1, 0, 2, 3)).reshape(frame_devs, token_count, -1)
+
     def gather_frames(values):
         full = lax.all_gather(values, "frame", axis=1, tiled=True)
         return full.reshape(group_count, values.shape[-1])
 
     def scatter_frames(values):
-        parts = values.reshape(clips, frame_devs, frames * per_frame_dev, width)
-        parts = jnp.transpose(parts, (1, 0, 2, 3)).reshape(group_count, width)
+        parts = to_frames(values).reshape(group_count, width)
         return lax.psum_scatter(parts, "frame", scatter_dimension=0, tiled=True).reshape(
             tokens.shape
         )
@@ -554,7 +740,15 @@
     mod_local = jnp.einsum(
         "cld,de->cle", silu_low, mod_weight, preferred_element_type=F32
     ) + mod_bias.astype(F32)
-    modulation = lax.all_gather(mod_local.astype(BF), "row", axis=2, tiled=True).astype(F32)
+    mod_width = mod_local.shape[2]
+    modulation = exchange(
+        "gather_mod",
+        "row",
+        0,
+        [(0, 0, all_of, lanes_at(mod_width))],
+        [mod_local.astype(BF).reshape(clips * frames, mod_width)],
+        [((clips * frames, mod_width * row_devs), BF)],
+    )[0].astype(F32)
     modulation = modulation.reshape(clips, frames, 6, 1, 1, width)
     shift_one, scale_one, gate_one, shift_two, scale_two, gate_two = [
         modulation[:, :, part] for part in range(6)
@@ -572,36 +766,44 @@
 
     token_f = tokens.astype(F32)
     hidden_one, norm_one_pull = jax.vjp(modulate, token_f, shift_one, scale_one)
-    hidden_group = gather_frames(hidden_one.astype(BF))
+    steps_wide = jnp.broadcast_to(timesteps.reshape(-1, 1), (clips * frames, LANES))
+    hidden_parts, steps_parts = gather(
+        "gather_one",
+        "frame",
+        1,
+        [hidden_one.astype(BF).reshape(token_count, width), steps_wide],
+    )
+    hidden_group = by_frames(hidden_parts)
 
     grad_out = cotangent.astype(F32)
     grad_branch_two = (grad_out * gate_two).astype(BF)
 
     pack, gate_raw = qkv_project(hidden_group, weight_in, cosines, sines, clips, heads)
 
-    def exchange(values):
-        return lax.all_to_all(values, "row", split_axis=0, concat_axis=0, tiled=True)
-
     half = tile // row_devs
     pairs = [(r, r ^ 1) for r in range(row_devs)]
 
-    def to_heads(packed, count):
-        parts = packed.reshape(row_devs, count, -1, per_frame_dev, LANES)
-        return jnp.transpose(parts, (1, 2, 0, 3, 4)).reshape(-1, LANES)
-
-    def to_tokens(values, count):
-        parts = values.reshape(count, -1, row_devs, per_frame_dev, LANES)
-        return jnp.transpose(parts, (2, 0, 1, 3, 4)).reshape(row_devs, count, half, LANES)
-
-    arrived = exchange(pack.reshape(row_devs, 6, half, LANES))
-    queries = to_heads(arrived[:, :2], 2)
-    own_half = to_heads(arrived[:, 2:], 4)
-    other_half = lax.ppermute(own_half, "row", pairs)
-    keys_values = jnp.where(
-        core == 0,
-        jnp.concatenate([own_half, other_half], axis=0),
-        jnp.concatenate([other_half, own_half], axis=0),
-    )
+    spans = half // per_frame_dev
+    by_token = (spans, per_frame_dev, LANES)
+    by_head = (spans, row_devs, per_frame_dev, LANES)
+
+    def peer_rows(ref, peer):
+        return ref.at[:, :, peer]
+
+    queries, keys_values = exchange(
+        "to_heads",
+        "row",
+        2,
+        [
+            (0, 0, lambda r, p: r.at[p, 0:2], lambda r, me, p: r.at[:, :, me]),
+            (0, 1, lambda r, p: r.at[p, 2:6], lambda r, me, p: r.at[p % 2, :, :, me]),
+        ],
+        [pack.reshape((row_devs, 6) + by_token)],
+        [((2,) + by_head, BF), ((2, 4) + by_head, BF)],
+        pair_of=1,
+    )
+    queries = queries.reshape(-1, LANES)
+    keys_values = keys_values.reshape(-1, LANES)
 
     rest = jnp.concatenate([out_weight, take_slice(up_weight, 1), take_slice(down_weight, 1)], 1)
     rest = lax.all_gather(rest, "row", axis=0, tiled=True)
@@ -612,24 +814,32 @@
 
     attended_heads, attended_t, lse = attend(queries, keys_values, tile, per_frame, scale)
     pack_shape = (clips, heads, 2, 2, half, LANES)
-    arrived = exchange(to_tokens(attended_heads, 2)).reshape(pack_shape)
+    (arrived,) = exchange(
+        "to_tokens",
+        "row",
+        3,
+        [(0, 0, peer_rows, at_sender)],
+        [attended_heads.reshape((2,) + by_head)],
+        [((row_devs, 2) + by_token, BF)],
+    )
+    arrived = arrived.reshape(pack_shape)
     gated_group, attended = gate_forward(arrived, gate_raw, clips, heads)
 
-    def group_split(values):
-        parts = values.reshape(clips, frame_devs, frames * per_frame_dev, slice_width)
-        parts = jnp.transpose(parts, (1, 0, 2, 3))
-        return parts.reshape(frame_devs, token_count, slice_width)
-
-    def group_join(values):
-        parts = values.reshape(frame_devs, clips, frames * per_frame_dev, slice_width)
-        return jnp.transpose(parts, (1, 0, 2, 3)).reshape(group_count, slice_width)
-
-    gated = lax.all_to_all(group_split(gated_group), "frame", 0, 0, tiled=True)
-    gated = jnp.transpose(gated, (1, 0, 2)).reshape(token_count, width)
+    (gated,) = exchange(
+        "gated_back",
+        "frame",
+        4,
+        [(0, 0, block_of, lanes_at(slice_width))],
+        [to_frames(gated_group)],
+        [((token_count, width), BF)],
+    )
     branch_one = jnp.dot(gated, full_out, preferred_element_type=F32).reshape(tokens.shape)
     after_one = token_f + gate_one * branch_one
     hidden_two, norm_two_pull = jax.vjp(modulate, after_one, shift_two, scale_two)
-    hidden_two_group = gather_frames(hidden_two.astype(BF))
+    (hidden_two_parts,) = gather(
+        "gather_two", "frame", 5, [hidden_two.astype(BF).reshape(token_count, width)]
+    )
+    hidden_two_group = by_frames(hidden_two_parts)
 
     pre_act = jnp.dot(hidden_two_group, weight_up, preferred_element_type=F32)
     act_values, gelu_pull = jax.vjp(partial(jax.nn.gelu, approximate=True), pre_act)
@@ -637,7 +847,9 @@
     grad_act = jnp.dot(grad_two_group, weight_down, preferred_element_type=F32)
     (grad_pre,) = gelu_pull(grad_act)
     grad_pre = grad_pre.astype(BF)
-    grad_hidden_two = scatter_frames(dot(grad_pre, weight_up, 1, 1).astype(BF)).astype(F32)
+    grad_hidden_two = scatter_sum(
+        "scatter_two", "frame", 6, to_frames(dot(grad_pre, weight_up, 1, 1).astype(BF))
+    ).reshape(tokens.shape)
     branch_two = scatter_frames(dot(act_low, weight_down, 1, 1).astype(BF)).astype(F32)
     mixed = (after_one + gate_two * branch_two).astype(BF)
     grad_gate_two = jnp.sum(grad_out * branch_two, axis=(2, 3), keepdims=True)
@@ -647,22 +859,32 @@
     grad_gate_one = jnp.sum(grad_after * branch_one, axis=(2, 3), keepdims=True)
     grad_branch_one = (grad_after * gate_one).astype(BF).reshape(token_count, width)
     grad_gated = dot(grad_branch_one, full_out, 1, 1).astype(BF)
-    grad_gated = jnp.transpose(
-        grad_gated.reshape(token_count, frame_devs, slice_width), (1, 0, 2)
-    )
-    grad_gated = group_join(lax.all_to_all(grad_gated, "frame", 0, 0, tiled=True))
+    (grad_gated,) = exchange(
+        "grad_gated",
+        "frame",
+        7,
+        [(0, 0, lanes_of(slice_width), at_sender)],
+        [grad_gated],
+        [((frame_devs, token_count, slice_width), BF)],
+    )
+    grad_gated = by_frames(grad_gated)
     down_pack, grad_gate = gate_back(grad_gated, gate_raw, attended, clips, heads)
-    downs = to_heads(exchange(down_pack.reshape(row_devs, 2, half, LANES)), 2)
-
-    mlp_grads = jnp.concatenate(
-        [
-            dot(hidden_two_group, grad_pre, 0, 0),
-            dot(grad_two_group, act_low, 0, 0),
-            dot(gated, grad_branch_one, 0, 0),
-        ],
-        axis=1,
-    ).astype(BF)
-    mlp_grads = lax.psum_scatter(mlp_grads, "row", scatter_dimension=0, tiled=True)
+    (downs,) = exchange(
+        "grad_to_heads",
+        "row",
+        8,
+        [(0, 0, block_of, lambda r, me, p: r.at[:, :, me])],
+        [down_pack.reshape((row_devs, 2) + by_token)],
+        [((2,) + by_head, BF)],
+    )
+    downs = downs.reshape(-1, LANES)
+
+    weight_grads = mlp_grads(
+        [(hidden_two_group, grad_pre), (grad_two_group, act_low), (gated, grad_branch_one)],
+        row_devs,
+    )
+    downs, weight_grads = lax.optimization_barrier((downs, weight_grads))
+    weight_grads = lax.psum_scatter(weight_grads, "row", scatter_dimension=0, tiled=True)
 
     grad_queries, grad_kv = attend_back(
         queries, downs, lse, attended_t, keys_values, tile, per_frame, scale
@@ -672,12 +894,25 @@
     give = lax.dynamic_index_in_dim(grad_kv, 1 - core, 0, keepdims=False)
     got = lax.ppermute(give, "row", pairs)
     grad_kv = (keep.astype(F32) + got.astype(F32)).astype(BF)
-    back_pack = jnp.concatenate([to_tokens(grad_queries, 2), to_tokens(grad_kv, 4)], axis=1)
-    back_pack = exchange(back_pack).reshape(clips, heads, 2, 6, half, LANES)
+    (back_pack,) = exchange(
+        "grad_to_tokens",
+        "row",
+        9,
+        [
+            (0, 0, peer_rows, lambda r, me, p: r.at[me, 0:2]),
+            (1, 0, peer_rows, lambda r, me, p: r.at[me, 2:6]),
+        ],
+        [grad_queries.reshape((2,) + by_head), grad_kv.reshape((4,) + by_head)],
+        [((row_devs, 6) + by_token, BF)],
+    )
+    back_pack = back_pack.reshape(clips, heads, 2, 6, half, LANES)
     grad_mixed, grad_hidden = qkv_back(
         back_pack, grad_gate, weight_in, cosines, sines, clips, heads
     )
-    grad_hidden_one = scatter_frames(grad_hidden).astype(F32)
+    grad_mixed, weight_grads = lax.optimization_barrier((grad_mixed, weight_grads))
+    grad_hidden_one = scatter_sum("scatter_one", "frame", 10, to_frames(grad_hidden)).reshape(
+        tokens.shape
+    )
     in_grad = lax.psum_scatter(
         dot(hidden_group, grad_mixed, 0, 0).astype(BF), "row", scatter_dimension=0, tiled=True
     )
@@ -696,15 +931,24 @@
         ],
         axis=2,
     ).reshape(clips * frames, 6 * width)
-    grad_mod = lax.psum_scatter(grad_mod, "row", scatter_dimension=1, tiled=True).astype(BF)
-    grad_mod_all = lax.all_gather(grad_mod, "frame", axis=0, tiled=True)
-    steps_all = lax.all_gather(timesteps.reshape(-1), "frame", axis=0, tiled=True)
+    grad_mod = jnp.transpose(
+        grad_mod.reshape(clips * frames, row_devs, mod_width), (1, 0, 2)
+    )
+    grad_mod = scatter_sum("scatter_mod", "row", 11, grad_mod, BF)
+    (grad_mod_all,) = gather("gather_grad_mod", "frame", 12, [grad_mod])
+    grad_mod_all = grad_mod_all.reshape(-1, mod_width)
+    steps_all = steps_parts.reshape(-1, LANES)[:, 0]
     hot_all = steps_all[:, None] == lax.broadcasted_iota(jnp.int32, (1, step_count), 1)
     embed_all = jnp.dot(hot_all.astype(BF), noise_table, preferred_element_type=F32)
     silu_all, silu_pull = jax.vjp(jax.nn.silu, embed_all)
     mod_weight_grad = dot(silu_all.astype(BF), grad_mod_all, 0, 0)
     mod_bias_grad = jnp.sum(grad_mod_all.astype(F32), axis=0)
-    grad_silu = lax.psum(dot(grad_mod_all, mod_weight, 1, 1), "row")
+    grad_silu = dot(grad_mod_all, mod_weight, 1, 1)
+    frame_count, cut = grad_silu.shape[0], width // row_devs
+    grad_silu = jnp.transpose(grad_silu.reshape(frame_count, row_devs, cut), (1, 0, 2))
+    grad_silu = scatter_sum("scatter_silu", "row", 13, grad_silu)
+    (grad_silu,) = gather("gather_silu", "row", 14, [grad_silu])
+    grad_silu = jnp.transpose(grad_silu, (1, 0, 2)).reshape(frame_count, width)
     (grad_embedding,) = silu_pull(grad_silu)
     noise_table_grad = lax.dot_general(
         hot_all.astype(F32),
@@ -713,16 +957,15 @@
         precision=lax.Precision.HIGHEST,
     )
 
-    hidden_slice = up_weight.shape[1] // frame_devs
-    up_part, down_part = mlp_grads[:, :hidden_slice], mlp_grads[:, hidden_slice : 2 * hidden_slice]
-    out_weight_grad = lax.psum(mlp_grads[:, 2 * hidden_slice :], "frame").astype(F32)
-    mlp_all = lax.all_gather(jnp.stack([up_part, down_part]), "frame", axis=0, tiled=False)
+    grads_all = lax.all_gather(weight_grads[0], "frame", axis=0, tiled=False)
 
     def join_columns(parts):
         return jnp.transpose(parts, (1, 0, 2)).reshape(parts.shape[1], -1).astype(F32)
 
-    up_weight_grad = join_columns(mlp_all[:, 0])
-    down_weight_grad = join_columns(mlp_all[:, 1])
+    hidden_slice = up_weight.shape[1] // frame_devs
+    up_weight_grad = join_columns(grads_all[:, :, :hidden_slice])
+    down_weight_grad = join_columns(grads_all[:, :, hidden_slice : 2 * hidden_slice])
+    out_weight_grad = jnp.sum(grads_all[:, :, 2 * hidden_slice :].astype(F32), axis=0)
     in_all = lax.all_gather(in_grad, "frame", axis=0, tiled=False)
     in_all = in_all.reshape(frame_devs, in_grad.shape[0], 4, slice_width)
     attn_in_grad = jnp.transpose(in_all, (1, 2, 0, 3)).reshape(attn_in.shape).astype(F32)

time: 952 us -> 604 us (0.63)
  waiting for transfers between devices: 431 us -> 41.6 us
  Pallas kernels: 110 us -> 413 us
  blocking collectives: 198 us -> 0 us
  other arithmetic: 49.6 us -> 26.3 us
  matrix products: 59 us -> 43.2 us
  starting transfers between devices: 16.6 us -> 2.03 us
    pallas_call x0 -> x16, Pallas kernels: none -> 303 us  [the longest x15 293 us: exchange(): pl.pallas_call(partial(exchange_kernel, axis, moves, len(arrays), len(sha...]
    all_to_all x5 -> x0, blocking collectives: 166 us -> none  [the longest x3 142 us: exchange(): lax.all_to_all(values, 'row', split_axis=0, concat_axis=0, tiled=True)]
    all_gather x3 -> x1, waiting for transfers between devices: 81.9 us -> 0.02 us  [gather_frames(): full = lax.all_gather(values, 'frame', axis=1, tiled=True)]
    reduce_scatter x3 -> x1, waiting for transfers between devices: 84 us -> 8.87 us  [scatter_frames(): lax.psum_scatter(parts, 'frame', scatter_dimension=0, tiled=True)]
    unnamed x16 -> x8, waiting for transfers between devices: 71 us -> 0.81 us
    psum x2 -> x0, waiting for transfers between devices: 66.8 us -> none  [the longest x1 35.3 us: on_device(): lax.psum(mlp_grads[:, 2 * hidden_slice:], 'frame').astype(F32)]
    all_gather x1, waiting for transfers between devices: 31.4 us -> 0.02 us  [on_device(): lax.all_gather(take_slice(attn_in, 4), 'row', axis=0, tiled=True)]
    all_gather x1, waiting for transfers between devices: 35 us -> 10.2 us  [on_device(): grads_all = lax.all_gather(weight_grads[0], 'frame', axis=0, tiled=False)]
  transfers between devices with their start and end apart: 18 -> 9, of which waited for: 16 -> 5; matrix products, arithmetic and copies ran while one was open for 13% -> 13% of each run, Pallas kernels for 4% -> 63%
where the time goes in v2:
time: 604 us; the launch traced here: 599 us
  Pallas kernels  413 us (68%)
  local copies, waits for them, and re-layouts  56.8 us (9%)
  matrix products  43.2 us (7%)
  waiting for transfers between devices  41.6 us (7%)
  other arithmetic  26.3 us (4%)
  between operations  15.5 us (3%)
    pallas_call x15, Pallas kernels, exchange(): pl.pallas_call(partial(exchange_kernel, axis, moves, len(arrays), len(sha...  293 us
    pallas_call x1, Pallas kernels, attend_back(): pl.pallas_call(partial(attend_back_kernel, tile, tile // 2, per_frame, sc...  58.4 us
    unnamed x113, local copies, waits for them, and re-layouts  34 us
    pallas_call x1, Pallas kernels, attend(): pl.pallas_call(partial(attend_kernel, tile, per_frame, scale), grid=(4,),...  32.6 us
    dot_general x6, matrix products, dot(): lax.dot_general(left, right, (((left_dim,), (right_dim,)), ((), ())), pre...  21.1 us
  transfers between devices with their start and end apart: 9, of which 5 were waited for; matrix products, arithmetic and copies ran while one was open for 13% of the time, Pallas kernels for 63%

profile of v2, /device:TPU:0, one launch (start us, length us, event | category | flops | bytes accessed | tf_op | source)
XLA Modules:
  0.0 598.8 jit_solution(17171234586760259010)
XLA Ops:
  22.8 9.4 %gather_mod.1 = bf16[8,6144]{1,0:T(8,128)(2,1)S(1)} custom-call(bf16[8,768]{1,0:T(8,128)(2,1)S(1)} %fusion.29.refs_0_), custom_call_target="tpu_custom_call" | custom-call | bytes 20368640 | tf_op jit(solution)/shard_map/gather_mod/pallas_call | solution.py:563
  35.3 27.2 %gather_one.1 = (bf16[4,256,1024]{2,1,0:T(8,128)(2,1)S(1)}, s32[4,8,128]{2,1,0:T(8,128)S(1)}) custom-call(bf16[256,1024]{1,0:T(8,128)(2,1)S(1)} %bitcast.174, s32[8,128]{1,0:T(8,128)S(1)} %broadcast_in_dim.10.refs_1_), custom_call_target="tpu_custom_call" | custom-call | bytes 35851520 | tf_op jit(solution)/shard_map/gather_one/pallas_call | solution.py:563
  67.8 5.1 qkv_project.1
  73.9 58.1 %to_heads.1 = (bf16[2,4,8,32,128]{4,3,2,1,0:T(8,128)(2,1)S(1)}, bf16[2,4,4,8,32,128]{5,4,3,2,1,0:T(8,128)(2,1)S(1)}) custom-call(bf16[8,6,4,32,128]{4,3,2,1,0:T(8,128)(2,1)S(1)} %bitcast.176), custom_call_target="tpu_custom_call" | custom-call | bytes 67185920 | tf_op jit(solution)/shard_map/to_heads/pallas_call | solution.py:563
  134.1 32.6 %attend.1 = (bf16[2048,128]{1,0:T(8,128)(2,1)}, bf16[2,128,1024]{2,1,0:T(8,128)(2,1)}, f32[4,1,1024]{2,1,0:T(1,128)}) custom-call(bf16[2048,128]{1,0:T(8,128)(2,1)} %bitcast.189, bf16[8192,128]{1,0:T(8,128)(2,1)} %bitcast.187), custom_call_target="tpu_custom_call" | custom-call | flops 20000000000 | bytes 8000000 | tf_op jit(solution)/shard_map/attend/pallas_call | solution.py:355
  167.8 24.8 %to_tokens.1 = bf16[8,2,4,32,128]{4,3,2,1,0:T(8,128)(2,1)S(1)} custom-call(bf16[2,4,8,32,128]{4,3,2,1,0:T(8,128)(2,1)S(1)} %bitcast.179), custom_call_target="tpu_custom_call" | custom-call | bytes 35728640 | tf_op jit(solution)/shard_map/to_tokens/pallas_call | solution.py:563
  193.5 3.8 gate_forward.1
  198.3 10.1 %gated_back.1.refs_4_ = bf16[256,1024]{1,0:T(8,128)(2,1)S(1)} custom-call(bf16[4,256,256]{2,1,0:T(8,128)(2,1)S(1)} %bitcast.180), custom_call_target="tpu_custom_call" | custom-call | bytes 35728640 | tf_op jit(solution)/shard_map/gated_back/pallas_call | solution.py:563
  211.9 26.2 %gather_two.1 = bf16[4,256,1024]{2,1,0:T(8,128)(2,1)S(1)} custom-call(bf16[256,1024]{1,0:T(8,128)(2,1)S(1)} %bitcast.166), custom_call_target="tpu_custom_call" | custom-call | bytes 35728640 | tf_op jit(solution)/shard_map/gather_two/pallas_call | solution.py:563
  238.2 5.0 multiply_convert_fusion
  248.3 7.9 %fusion.6.refs_1_ = bf16[1024,1024]{1,0:T(8,128)(2,1)S(1)} fusion(f32[1024,1024]{1,0:T(8,128)} %get-tuple-element.100, bf16[1024,1024]{1,0:T(8,128)(2,1)} %bitcast.211, bf16[1024,3072]{1,0:T(8,128)(2,1)} %all-gather.9.cloned.1.call-done), kind=kOutput, calls=%fused_computation.8 | convolution fusion | flops 2168455168 | bytes 10485760 | tf_op jit(solution)/shard_map/dot_general | solution.py:847
  256.2 4.7 convolution_convert_fusion.1
  261.0 31.6 %scatter_two.1 = f32[256,1024]{1,0:T(8,128)S(1)} custom-call(bf16[4,256,1024]{2,1,0:T(8,128)(2,1)S(1)} %bitcast.171), custom_call_target="tpu_custom_call" | custom-call | bytes 82914560 | tf_op jit(solution)/shard_map/scatter_two/pallas_call | solution.py:563
  293.1 8.9 %reduce-scatter.4.cloned.1.call-done = bf16[256,1024]{1,0:T(8,128)(2,1)} async-done(((bf16[1024,1024]{1,0:T(8,128)(2,1)}), bf16[256,1024]{1,0:T(8,128)(2,1)}) %reduce-scatter.4.cloned.1.call-update) | async-done | bytes 524304 | tf_op jit(solution)/shard_map/reduce_scatter | solution.py:725
  311.0 10.7 %mlp_grads.1 = bf16[8,128,3072]{2,1,0:T(8,128)(2,1)} custom-call(bf16[1024,1024]{1,0:T(8,128)(2,1)S(1)} %bitcast.168, bf16[1024,1024]{1,0:T(8,128)(2,1)S(1)} %copy-done.26, bf16[1024,1024]{1,0:T(8,128)(2,1)} %bitcast.212, bf16[1024,1024]{1,0:T(8,128)(2,1)} %copy-done.47, bf16[256,1024]{1,0:T(8,128)(2,1)S(1)} %copy-done.15, bf16[256,1024]{1,0:T(8,128)(2,1)S(1)} %bitcast.182), custom_call_target="tpu_custom_call" | custom-call | flops 5000000000 | bytes 18000000 | tf_op jit(solution)/shard_map/mlp_grads/pallas_call | solution.py:665
  324.9 9.0 %grad_gated.1 = bf16[4,256,256]{2,1,0:T(8,128)(2,1)S(1)} custom-call(bf16[256,1024]{1,0:T(8,128)(2,1)S(1)} %fusion.24.refs_0_), custom_call_target="tpu_custom_call" | custom-call | bytes 35728640 | tf_op jit(solution)/shard_map/grad_gated/pallas_call | solution.py:563
  334.7 3.8 gate_back.1
  339.6 12.5 %grad_to_heads.1 = bf16[2,4,8,32,128]{4,3,2,1,0:T(8,128)(2,1)S(1)} custom-call(bf16[8,2,4,32,128]{4,3,2,1,0:T(8,128)(2,1)S(1)} %bitcast.178), custom_call_target="tpu_custom_call" | custom-call | bytes 35728640 | tf_op jit(solution)/shard_map/grad_to_heads/pallas_call | solution.py:563
  352.9 58.4 %attend_back.1 = (bf16[2048,128]{1,0:T(8,128)(2,1)}, bf16[8192,128]{1,0:T(8,128)(2,1)}) custom-call(bf16[2048,128]{1,0:T(8,128)(2,1)} %bitcast.190, bf16[2048,128]{1,0:T(8,128)(2,1)} %bitcast.177, f32[4,1,1024]{2,1,0:T(1,128)} %get-tuple-element.40.lse_ref, bf16[2,128,1024]{2,1,0:T(8,128)(2,1)} %get-tuple-element.41.out_t_ref, bf16[8192,128]{1,0:T(8,128)(2,1)} %bitcast.188), custom_call_target="tpu_custom_call" | custom-call | flops 49999998976 | bytes 12000000 | tf_op jit(solution)/shard_map/attend_back/pallas_call | solution.py:471
  419.2 31.1 %grad_to_tokens.1 = bf16[8,6,4,32,128]{4,3,2,1,0:T(8,128)(2,1)S(1)} custom-call(bf16[2,4,8,32,128]{4,3,2,1,0:T(8,128)(2,1)S(1)} %bitcast.181, bf16[4,4,8,32,128]{4,3,2,1,0:T(8,128)(2,1)S(1)} %bitcast.165), custom_call_target="tpu_custom_call" | custom-call | bytes 67185920 | tf_op jit(solution)/shard_map/grad_to_tokens/pallas_call | solution.py:563
  450.4 6.5 %qkv_back.1 = (bf16[1024,1024]{1,0:T(8,128)(2,1)S(1)}, bf16[1024,1024]{1,0:T(8,128)(2,1)}) custom-call(bf16[1,4,2,6,128,128]{5,4,3,2,1,0:T(8,128)(2,1)S(1)} %bitcast.164, bf16[1024,256]{1,0:T(8,128)(2,1)S(1)} %copy-done.13, bf16[1024,1024]{1,0:T(8,128)(2,1)} %all-gather.7.cloned.1.call-done.w_ref, f32[1024,128]{1,0:T(8,128)S(1)} %copy-done.4, ...), custom_call_target="tpu_custom_call" | custom-call | tf_op jit(solution)/shard_map/qkv_back/pallas_call | solution.py:183
  458.2 5.9 convolution_convert_fusion
  468.1 27.2 %scatter_one.1 = f32[256,1024]{1,0:T(8,128)S(1)} custom-call(bf16[4,256,1024]{2,1,0:T(8,128)(2,1)S(1)} %bitcast.170), custom_call_target="tpu_custom_call" | custom-call | bytes 82914560 | tf_op jit(solution)/shard_map/scatter_one/pallas_call | solution.py:563
  500.5 7.7 %reduce-scatter.8.cloned.1.call-done = bf16[128,1024]{1,0:T(8,128)(2,1)} async-done(((bf16[1024,1024]{1,0:T(8,128)(2,1)}), bf16[128,1024]{1,0:T(8,128)(2,1)}) %reduce-scatter.8.cloned.1.call-update) | async-done | bytes 262160 | tf_op jit(solution)/shard_map/reduce_scatter | solution.py:916
  508.2 6.9 %scatter_mod.1.refs_0_ = bf16[8,768]{1,0:T(8,128)(2,1)S(1)} custom-call(f32[8,8,768]{2,1,0:T(8,128)S(1)} %bitcast.185), custom_call_target="tpu_custom_call" | custom-call | bytes 25898240 | tf_op jit(solution)/shard_map/scatter_mod/pallas_call | solution.py:563
  515.1 5.4 gather_grad_mod.1
  522.5 6.3 %scatter_silu.1.refs_0_ = f32[32,128]{1,0:T(8,128)S(1)} custom-call(f32[8,32,128]{2,1,0:T(8,128)S(1)} %convolution_bitcast_fusion.refs_0_), custom_call_target="tpu_custom_call" | custom-call | bytes 23932160 | tf_op jit(solution)/shard_map/scatter_silu/pallas_call | solution.py:563
  528.8 6.9 %gather_silu.1 = f32[8,32,128]{2,1,0:T(8,128)S(1)} custom-call(f32[32,128]{1,0:T(8,128)S(1)} %scatter_silu.1.refs_0_), custom_call_target="tpu_custom_call" | custom-call | bytes 20491520 | tf_op jit(solution)/shard_map/gather_silu/pallas_call | solution.py:563
  538.6 3.9 fusion.45
  542.4 10.2 %all-gather.13.cloned.1.call-done = bf16[4,128,3072]{2,1,0:T(8,128)(2,1)} async-done(((bf16[1,128,3072]{2,1,0:T(8,128)(2,1)}), bf16[4,128,3072]{2,1,0:T(8,128)(2,1)}) %all-gather.13.cloned.1.call-update) | async-done | bytes 3145744 | tf_op jit(solution)/shard_map/all_gather | solution.py:960
  569.8 11.2 %all-gather.15.cloned.1.call-done = bf16[512,1024]{1,0:T(8,128)(2,1)} async-done(((bf16[128,1024]{1,0:T(8,128)(2,1)}), bf16[512,1024]{1,0:T(8,128)(2,1)}) %all-gather.15.cloned.1.call-update) | async-done | bytes 1048592 | tf_op jit(solution)/shard_map/all_gather | solution.py:969
  583.9 4.3 copy.63
  (195 shorter events, 100.3 us)
Async XLA Ops:
  7.2 13.3 %copy-start = (bf16[1000,1024]{1,0:T(8,128)(2,1)S(1)}, bf16[1000,1024]{1,0:T(8,128)(2,1)}, u32[]{:S(2)}) copy-start(bf16[1000,1024]{1,0:T(8,128)(2,1)} %param.16) | copy-start | bytes 6144004
  7.2 58.6 %all-gather.7.cloned.1.call-start = ((), (), s32[]{:S(2)}) async-start(), calls=%async_computation.3 | async-start | bytes 2359296 | tf_op jit(solution)/shard_map/all_gather | solution.py:734
  11.6 196.8 %all-gather.9.cloned.1.call-start = ((), (), s32[]{:S(2)}) async-start(), calls=%async_computation.4 | async-start | bytes 7077888 | tf_op jit(solution)/shard_map/all_gather | solution.py:809
  15.6 4.9 copy-start.41
  15.6 4.9 copy-start.42
  20.4 227.9 %all-gather.11.cloned.1.call-start = ((), (), s32[]{:S(2)}) async-start(), calls=%async_computation.6 | async-start | bytes 2621440 | tf_op jit(solution)/shard_map/all_gather | solution.py:720
  20.5 11.8 %copy-start.33 = (bf16[1,8,2,16,1024]{4,3,2,1,0:T(8,128)(2,1)S(1)}, bf16[1,8,2,16,1024]{4,3,2,1,0:T(8,128)(2,1)}, u32[]{:S(2)}) copy-start(bf16[1,8,2,16,1024]{4,3,2,1,0:T(8,128)(2,1)} %param.23) | copy-start | bytes 1572868
  22.8 11.1 %copy-start.29 = (bf16[1,8,2,16,1024]{4,3,2,1,0:T(8,128)(2,1)S(1)}, bf16[1,8,2,16,1024]{4,3,2,1,0:T(8,128)(2,1)}, u32[]{:S(2)}) copy-start(bf16[1,8,2,16,1024]{4,3,2,1,0:T(8,128)(2,1)} %param.14) | copy-start | bytes 1572868
  32.3 31.4 %copy-start.43 = (f32[128]{0:T(128)S(1)}, f32[128]{0:T(128)}, u32[]{:S(2)}) copy-start(f32[128]{0:T(128)} %constant.85.clone) | copy-start | bytes 1540
  32.3 31.4 %copy-start.44 = (f32[128]{0:T(128)S(1)}, f32[128]{0:T(128)}, u32[]{:S(2)}) copy-start(f32[128]{0:T(128)} %constant.84.clone) | copy-start | bytes 1540
  32.3 31.4 %copy-start.45 = (f32[128]{0:T(128)S(1)}, f32[128]{0:T(128)}, u32[]{:S(2)}) copy-start(f32[128]{0:T(128)} %constant.83.clone) | copy-start | bytes 1540
  32.4 31.4 %copy-start.46 = (f32[128]{0:T(128)S(1)}, f32[128]{0:T(128)}, u32[]{:S(2)}) copy-start(f32[128]{0:T(128)} %constant.82.clone) | copy-start | bytes 1540
  33.3 268.7 %reduce-scatter.4.cloned.1.call-start = ((), (), s32[]{:S(2)}) async-start(), calls=%async_computation.5 | async-start | bytes 2621440 | tf_op jit(solution)/shard_map/reduce_scatter | solution.py:725
  65.8 7.1 %copy-start.1 = (f32[1024,128]{1,0:T(8,128)}, f32[1024,128]{1,0:T(8,128)S(1)}, u32[]{:S(2)}) copy-start(f32[1024,128]{1,0:T(8,128)S(1)} %get-tuple-element.97.sin_ref) | copy-start | bytes 1572868
  65.8 7.1 %copy-start.3 = (f32[1024,128]{1,0:T(8,128)}, f32[1024,128]{1,0:T(8,128)S(1)}, u32[]{:S(2)}) copy-start(f32[1024,128]{1,0:T(8,128)S(1)} %get-tuple-element.98.cos_ref) | copy-start | bytes 1572868
  208.4 29.8 %slice-start = ((s8[6291456]{0:T(1024)(128)(4,1)}), s8[4194304]{0:T(1024)(128)(4,1)S(1)}, s32[]{:S(2)}) async-start(s8[6291456]{0:T(1024)(128)(4,1)} %bitcast.209), calls=%async_computation.11 | async-start | bytes 8388608
  210.9 27.2 %slice-start.1 = ((s8[6291456]{0:T(1024)(128)(4,1)}), s8[2097152]{0:T(1024)(128)(4,1)S(1)}, s32[]{:S(2)}) async-start(s8[6291456]{0:T(1024)(128)(4,1)} %bitcast.209), calls=%async_computation.12 | async-start | bytes 4194304
  211.2 26.9 %copy-start.27 = (f32[1,8,2,16,1024]{4,3,2,0,1:T(8,128)}, f32[1,8,2,16,1024]{4,3,2,0,1:T(8,128)S(1)}, u32[]{:S(2)}) copy-start(f32[1,8,2,16,1024]{4,3,2,0,1:T(8,128)S(1)} %get-tuple-element.85) | copy-start | bytes 3145732
  238.1 5.0 copy-start.6
  248.2 209.9 %reduce-scatter.6.cloned.1.call-start = ((), (), s32[]{:S(2)}) async-start(), calls=%async_computation.7 | async-start | bytes 7077888 | tf_op jit(solution)/shard_map/reduce_scatter | solution.py:887
  256.2 4.7 copy-start.25
  261.0 31.7 %copy-start.28 = (f32[1,8,2,16,1024]{4,3,2,0,1:T(8,128)S(1)}, f32[1,8,2,16,1024]{4,3,2,0,1:T(8,128)}, u32[]{:S(2)}) copy-start(f32[1,8,2,16,1024]{4,3,2,0,1:T(8,128)} %copy-done.27) | copy-start | bytes 3145732
  352.9 155.3 %reduce-scatter.8.cloned.1.call-start = ((), (), s32[]{:S(2)}) async-start(), calls=%async_computation.8 | async-start | bytes 2359296 | tf_op jit(solution)/shard_map/reduce_scatter | solution.py:916
  413.6 3.7 collective-permute-start
  414.6 4.6 copy-start.20
  419.2 31.2 %copy-start.2 = (f32[1024,128]{1,0:T(8,128)S(1)}, f32[1024,128]{1,0:T(8,128)}, u32[]{:S(2)}) copy-start(f32[1024,128]{1,0:T(8,128)} %copy-done.1) | copy-start | bytes 1572868
  419.2 31.2 %copy-start.4 = (f32[1024,128]{1,0:T(8,128)S(1)}, f32[1024,128]{1,0:T(8,128)}, u32[]{:S(2)}) copy-start(f32[1024,128]{1,0:T(8,128)} %copy-done.3) | copy-start | bytes 1572868
  419.2 31.2 %copy-start.13 = (bf16[1024,256]{1,0:T(8,128)(2,1)S(1)}, bf16[1024,256]{1,0:T(8,128)(2,1)}, u32[]{:S(2)}) copy-start(bf16[1024,256]{1,0:T(8,128)(2,1)} %get-tuple-element.44.dgate_ref) | copy-start | bytes 1572868
  464.1 88.5 %all-gather.13.cloned.1.call-start = ((), (), s32[]{:S(2)}) async-start(), calls=%async_computation.9 | async-start | bytes 3932160 | tf_op jit(solution)/shard_map/all_gather | solution.py:960
  464.9 116.1 %all-gather.15.cloned.1.call-start = ((), (), s32[]{:S(2)}) async-start(), calls=%async_computation.10 | async-start | bytes 1310720 | tf_op jit(solution)/shard_map/all_gather | solution.py:969
  465.2 30.1 %copy-start.39 = (s32[32,1]{0,1:T(1,128)}, s32[32,1]{0,1:T(1,128)S(1)}, u32[]{:S(2)}) copy-start(s32[32,1]{0,1:T(1,128)S(1)} %copy.71) | copy-start | bytes 388
  522.5 16.1 %copy-start.40 = (s32[32,1]{0,1:T(1,128)S(1)}, s32[32,1]{0,1:T(1,128)}, u32[]{:S(2)}) copy-start(s32[32,1]{0,1:T(1,128)} %copy-done.39) | copy-start | bytes 388
  (27 other events, 46.2 us)
Sparse Core Ops, SparseCore 0:
  11.8 34.4 all-gather.6
  48.4 96.1 all-gather.8
  147.1 33.3 all-gather.10
  248.3 53.5 reduce-scatter.3
  353.0 71.9 reduce-scatter.5
  464.2 43.8 reduce-scatter.7
  510.0 42.5 all-gather.12
  554.5 26.4 all-gather.14
